TPU v7x, 128 devices: a whole 4x4x4 slice. The times are simulated.
128 devices in a mesh: section: 8 (over z, core), rows: 16 (over y, x).
Axes of the slice: x: 4, y: 4, z: 4, core: 2. Of those that a mesh axis runs over, the one named last changes fastest.
Arguments:
- features: bfloat16 [2048, 1536], P('rows'), may hold values from -6 to 6
- ages: int32 [2048], P('rows'), may hold values from 0 to 15
- age_table: bfloat16 [16, 1536], replicated, may hold values from -3 to 3
- returns: float32 [2048], P('rows'), may hold values from -6 to 6
- owners: int32 [2048, 1], P('rows'), may hold values from 0 to 15; in each aligned block of 128 rows (0 to 127, 128 to 255, ...) at most 32 rows name the same one
- slots: int32 [2048], P('rows'), may hold values from 0 to 4095
- norm_gain: float32 [8, 1536], P('section'), may hold values from 0.1 to 1.9
- w_gate: bfloat16 [8, 1536, 8960], P('section', None, 'rows'), may hold values from -0.15625 to 0.15625
- w_up: bfloat16 [8, 1536, 8960], P('section', None, 'rows'), may hold values from -0.15625 to 0.15625
- w_down: bfloat16 [8, 8960, 1536], P('section', 'rows'), may hold values from -0.0625 to 0.0625
- final_gain: float32 [1536], replicated, may hold values from 0.1 to 1.9
- reward_head: float32 [1536], replicated, may hold values from -0.15625 to 0.15625
- old_priority: float32 [65536], P('rows'), may hold values from 0.05 to 2
Outputs:
- rewards: float32 [2048], P(('rows', 'section'))
- weights: float32 [65536], P(('rows', 'section'))
Inputs may be any that keep to these rules, and one draw needn't show every extreme that they name: `owners`: among the rows of one device at most 32 name the same owner; in every draw some owner is named by exactly 32 rows of some device.
All inputs are finite; a program needn't handle non-finite values.
Results may differ from a plain program's by a relative error of at most 0.04.
Values may be sent and summed in bfloat16 or wider, within the bound.
A program may use at most 64 MiB of HBM per device.

v0:
```python
import jax
import jax.numpy as jnp
from jax import lax
from jax.sharding import PartitionSpec as P

MICRO = 8
CAP = 32


def joined_along(parts, dim):
    parts = jnp.moveaxis(parts, 0, dim)
    dims = parts.shape
    return parts.reshape(*dims[:dim], dims[dim] * dims[dim + 1], *dims[dim + 2 :])


def from_everyone(shard, axis):
    copies = jnp.broadcast_to(shard, (lax.axis_size(axis), *shard.shape))
    return lax.all_to_all(copies, axis, split_axis=0, concat_axis=0, tiled=True)


def gathered_copies(shard, axis, dim):
    return joined_along(from_everyone(shard, axis), dim)


def cut_along(shard, dim, count):
    dims = shard.shape
    parts = shard.reshape(*dims[:dim], count, dims[dim] // count, *dims[dim + 1 :])
    return jnp.moveaxis(parts, dim, 0)


def summed_on_arrival(shard, axis, dim):
    count = lax.axis_size(axis)
    parts = lax.all_to_all(cut_along(shard, dim, count), axis, 0, 0, tiled=True)
    return jnp.sum(parts.astype(jnp.float32), axis=0)


def shifted(value, axis, steps):
    count = lax.axis_size(axis)
    first, last = (max(0, -steps), min(count, count - steps))
    return lax.ppermute(value, axis, [(source, source + steps) for source in range(first, last)])


def from_root(shard, axis, root):
    return lax.dynamic_index_in_dim(lax.all_gather(shard, axis), root, 0, keepdims=False)


def of_everyone(shard, axis):
    everything = from_everyone(shard, axis)
    return jnp.sum(everything, axis=0)


def scaled_norm(values, gain):
    return values * lax.rsqrt(jnp.mean(values * values, axis=-1, keepdims=True) + 1e-06) * gain


def on_device(
    features,
    ages,
    age_table,
    returns,
    owners,
    slots,
    norm_gain,
    w_gate,
    w_up,
    w_down,
    final_gain,
    reward_head,
    old_priority,
):
    sections = lax.axis_size("section")
    section_now = lax.axis_index("section")
    groups = lax.axis_size("rows")
    rows_here = features.shape[0]
    block = rows_here // MICRO
    width = features.shape[1]
    table_size = old_priority.shape[0]
    onehot = (ages[:, None] == jnp.arange(age_table.shape[0])[None, :]).astype(jnp.bfloat16)
    entry = (
        features.astype(jnp.float32)
        + jnp.dot(onehot, age_table, preferred_element_type=jnp.float32)
    ).astype(jnp.bfloat16)

    def layer_split(state, layer):
        wide = state.astype(jnp.float32)
        normed = scaled_norm(wide, norm_gain[layer]).astype(jnp.bfloat16)
        piece = gathered_copies(normed, "rows", 0)
        gate = jnp.dot(piece, w_gate[layer], preferred_element_type=jnp.float32)
        upper = jnp.dot(piece, w_up[layer], preferred_element_type=jnp.float32)
        hidden = (jax.nn.silu(gate) * upper).astype(jnp.bfloat16)
        summed = summed_on_arrival(
            jnp.dot(hidden, w_down[layer], preferred_element_type=jnp.float32).astype(jnp.bfloat16),
            "rows",
            0,
        )
        return (wide + summed).astype(jnp.bfloat16)

    def tick(carry, step):
        current, collected = carry
        pick = jnp.minimum(step, MICRO - 1)
        block_in = lax.dynamic_slice_in_dim(entry, pick * block, block, 0)
        state = jnp.where(section_now == 0, block_in, current)
        state = layer_split(state, 0)
        finished_block = step - (sections - 1)
        valid = jnp.logical_and(section_now == sections - 1, finished_block >= 0)
        placed = lax.dynamic_update_slice_in_dim(
            collected, state, jnp.maximum(finished_block, 0) * block, 0
        )
        collected = jnp.where(valid, placed, collected)
        current = shifted(state, "section", 1)
        return ((current, collected), None)

    start_state = jnp.zeros((block, width), jnp.bfloat16)
    start_rows = jnp.zeros((rows_here, width), jnp.bfloat16)
    (unused_state, collected), unused_out = lax.scan(
        tick, (start_state, start_rows), jnp.arange(MICRO + sections - 1)
    )
    finished = scaled_norm(collected.astype(jnp.float32), final_gain)
    rewards_here = jnp.sum(finished * reward_head, axis=-1)
    rewards_here = from_root(rewards_here, "section", sections - 1)
    priority = jnp.exp(0.6 * jnp.log(jnp.abs(rewards_here - returns) + 0.05))
    owner = owners[:, 0]
    entries = jnp.arange(table_size)
    owner_hits = (owner[:, None] == jnp.arange(groups)[None, :]).astype(jnp.int32)
    rank = jnp.sum(jnp.cumsum(owner_hits, axis=0) * owner_hits, axis=1) - 1
    position = owner * CAP + rank
    send_values = jnp.zeros((groups * CAP,), jnp.float32).at[position].set(priority)
    send_places = (
        jnp.full((groups * CAP,), -1.0, jnp.float32).at[position].set(slots.astype(jnp.float32))
    )
    got_values, got_places = (
        lax.all_to_all(send_values, "rows", split_axis=0, concat_axis=0, tiled=True),
        lax.all_to_all(send_places, "rows", split_axis=0, concat_axis=0, tiled=True),
    )
    match = got_places[:, None] == entries[None, :].astype(jnp.float32)
    best = jnp.max(jnp.where(match, got_values[:, None], 0.0), axis=0)
    refreshed = jnp.where(best > 0.0, best, old_priority)
    total = of_everyone(jnp.sum(refreshed), "rows")
    weights = refreshed * (table_size * groups / total)
    reward_part = rows_here // sections
    weight_part = table_size // sections
    rewards_out = lax.dynamic_slice_in_dim(rewards_here, section_now * reward_part, reward_part, 0)
    weights_out = lax.dynamic_slice_in_dim(weights, section_now * weight_part, weight_part, 0)
    return (rewards_out, weights_out)


def solution(mesh):
    placed = (
        P("rows", None),
        P("rows"),
        P(),
        P("rows"),
        P("rows", None),
        P("rows"),
        P("section", None),
        P("section", None, "rows"),
        P("section", None, "rows"),
        P("section", "rows", None),
        P(),
        P(),
        P("rows"),
    )
    return jax.shard_map(
        on_device,
        mesh=mesh,
        in_specs=placed,
        out_specs=(P(("rows", "section")), P(("rows", "section"))),
        check_vma=False,
    )
```

profile of v0, /device:TPU:1, one launch (start us, length us, event | category | flops | bytes accessed | tf_op | source)
XLA Modules:
  0.0 775.6 jit_solution(13807824349384603526)
XLA Ops:
  3.6 722.4 %while.14 = (s32[]{:T(128)}, bf16[16,1536]{1,0:T(8,128)(2,1)S(1)}, bf16[128,1536]{1,0:T(8,128)(2,1)}, pred[]{:T(512)}, s32[15]{0:T(128)S(1)}, /*index=5*/bf16[12...) while((s32[]{:T(128)}, bf16[16,1536]{1,0:T(8,128)(2,1)S(1)}, ...), condition=%wide.region_3.4_spmd, body=%wide.region_0.3_spmd.sunk | while | flops 1323515904 | bytes 25103084 | solution.py:115
  6.0 20.9 %all_to_all.42 = bf16[16,16,1536]{2,1,0:T(8,128)(2,1)S(1)} all-to-all(bf16[16,16,1536]{2,1,0:T(8,128)(2,1)S(1)} %broadcast_in_dim.62), channel_id=1, replica_groups=mesh['section'=8,'rows'=16] {'rows'}, dimensions={0} | all-to-all | bytes 1572864 | tf_op jit(solution)/shard_map/while/body/eval_jaxpr/all_to_all | solution.py:18
  27.6 5.1 convolution_convert_fusion.2
  32.7 3.7 all-to-all-start.1
  37.1 12.0 %all-to-all-done.1 = bf16[16,16,1536]{2,1,0:T(8,128)(2,1)S(1)} async-done(((bf16[16,16,1536]{2,1,0:T(8,128)(2,1)}), bf16[16,16,1536]{2,1,0:T(8,128)(2,1)S(1)}, u32[]{:S(2)}, u32[]{:S(2)}) %all-to-all-start.1) | async-done | bytes 786464 | tf_op jit(solution)/shard_map/while/body/eval_jaxpr/all_to_all | solution.py:33
  50.7 6.1 collective-permute-start
  60.3 15.8 %all_to_all.42 = bf16[16,16,1536]{2,1,0:T(8,128)(2,1)S(1)} all-to-all(bf16[16,16,1536]{2,1,0:T(8,128)(2,1)S(1)} %broadcast_in_dim.62), channel_id=1, replica_groups=mesh['section'=8,'rows'=16] {'rows'}, dimensions={0} | all-to-all | bytes 1572864 | tf_op jit(solution)/shard_map/while/body/eval_jaxpr/all_to_all | solution.py:18
  76.7 5.1 convolution_convert_fusion.2
  81.8 3.7 all-to-all-start.1
  86.2 14.8 %all-to-all-done.1 = bf16[16,16,1536]{2,1,0:T(8,128)(2,1)S(1)} async-done(((bf16[16,16,1536]{2,1,0:T(8,128)(2,1)}), bf16[16,16,1536]{2,1,0:T(8,128)(2,1)S(1)}, u32[]{:S(2)}, u32[]{:S(2)}) %all-to-all-start.1) | async-done | bytes 786464 | tf_op jit(solution)/shard_map/while/body/eval_jaxpr/all_to_all | solution.py:33
  102.6 3.8 collective-permute-start
  109.9 16.2 %all_to_all.42 = bf16[16,16,1536]{2,1,0:T(8,128)(2,1)S(1)} all-to-all(bf16[16,16,1536]{2,1,0:T(8,128)(2,1)S(1)} %broadcast_in_dim.62), channel_id=1, replica_groups=mesh['section'=8,'rows'=16] {'rows'}, dimensions={0} | all-to-all | bytes 1572864 | tf_op jit(solution)/shard_map/while/body/eval_jaxpr/all_to_all | solution.py:18
  126.7 5.1 convolution_convert_fusion.2
  131.9 3.7 all-to-all-start.1
  136.3 15.4 %all-to-all-done.1 = bf16[16,16,1536]{2,1,0:T(8,128)(2,1)S(1)} async-done(((bf16[16,16,1536]{2,1,0:T(8,128)(2,1)}), bf16[16,16,1536]{2,1,0:T(8,128)(2,1)S(1)}, u32[]{:S(2)}, u32[]{:S(2)}) %all-to-all-start.1) | async-done | bytes 786464 | tf_op jit(solution)/shard_map/while/body/eval_jaxpr/all_to_all | solution.py:33
  158.7 16.7 %all_to_all.42 = bf16[16,16,1536]{2,1,0:T(8,128)(2,1)S(1)} all-to-all(bf16[16,16,1536]{2,1,0:T(8,128)(2,1)S(1)} %broadcast_in_dim.62), channel_id=1, replica_groups=mesh['section'=8,'rows'=16] {'rows'}, dimensions={0} | all-to-all | bytes 1572864 | tf_op jit(solution)/shard_map/while/body/eval_jaxpr/all_to_all | solution.py:18
  176.1 5.1 convolution_convert_fusion.2
  181.2 3.7 all-to-all-start.1
  185.6 12.3 %all-to-all-done.1 = bf16[16,16,1536]{2,1,0:T(8,128)(2,1)S(1)} async-done(((bf16[16,16,1536]{2,1,0:T(8,128)(2,1)}), bf16[16,16,1536]{2,1,0:T(8,128)(2,1)S(1)}, u32[]{:S(2)}, u32[]{:S(2)}) %all-to-all-start.1) | async-done | bytes 786464 | tf_op jit(solution)/shard_map/while/body/eval_jaxpr/all_to_all | solution.py:33
  206.2 16.6 %all_to_all.42 = bf16[16,16,1536]{2,1,0:T(8,128)(2,1)S(1)} all-to-all(bf16[16,16,1536]{2,1,0:T(8,128)(2,1)S(1)} %broadcast_in_dim.62), channel_id=1, replica_groups=mesh['section'=8,'rows'=16] {'rows'}, dimensions={0} | all-to-all | bytes 1572864 | tf_op jit(solution)/shard_map/while/body/eval_jaxpr/all_to_all | solution.py:18
  223.5 5.1 convolution_convert_fusion.2
  228.6 3.7 all-to-all-start.1
  233.0 12.2 %all-to-all-done.1 = bf16[16,16,1536]{2,1,0:T(8,128)(2,1)S(1)} async-done(((bf16[16,16,1536]{2,1,0:T(8,128)(2,1)}), bf16[16,16,1536]{2,1,0:T(8,128)(2,1)S(1)}, u32[]{:S(2)}, u32[]{:S(2)}) %all-to-all-start.1) | async-done | bytes 786464 | tf_op jit(solution)/shard_map/while/body/eval_jaxpr/all_to_all | solution.py:33
  253.6 16.7 %all_to_all.42 = bf16[16,16,1536]{2,1,0:T(8,128)(2,1)S(1)} all-to-all(bf16[16,16,1536]{2,1,0:T(8,128)(2,1)S(1)} %broadcast_in_dim.62), channel_id=1, replica_groups=mesh['section'=8,'rows'=16] {'rows'}, dimensions={0} | all-to-all | bytes 1572864 | tf_op jit(solution)/shard_map/while/body/eval_jaxpr/all_to_all | solution.py:18
  271.0 5.1 convolution_convert_fusion.2
  276.1 3.7 all-to-all-start.1
  280.5 12.2 %all-to-all-done.1 = bf16[16,16,1536]{2,1,0:T(8,128)(2,1)S(1)} async-done(((bf16[16,16,1536]{2,1,0:T(8,128)(2,1)}), bf16[16,16,1536]{2,1,0:T(8,128)(2,1)S(1)}, u32[]{:S(2)}, u32[]{:S(2)}) %all-to-all-start.1) | async-done | bytes 786464 | tf_op jit(solution)/shard_map/while/body/eval_jaxpr/all_to_all | solution.py:33
  301.1 16.7 %all_to_all.42 = bf16[16,16,1536]{2,1,0:T(8,128)(2,1)S(1)} all-to-all(bf16[16,16,1536]{2,1,0:T(8,128)(2,1)S(1)} %broadcast_in_dim.62), channel_id=1, replica_groups=mesh['section'=8,'rows'=16] {'rows'}, dimensions={0} | all-to-all | bytes 1572864 | tf_op jit(solution)/shard_map/while/body/eval_jaxpr/all_to_all | solution.py:18
  318.5 5.1 convolution_convert_fusion.2
  323.6 3.7 all-to-all-start.1
  328.0 12.2 %all-to-all-done.1 = bf16[16,16,1536]{2,1,0:T(8,128)(2,1)S(1)} async-done(((bf16[16,16,1536]{2,1,0:T(8,128)(2,1)}), bf16[16,16,1536]{2,1,0:T(8,128)(2,1)S(1)}, u32[]{:S(2)}, u32[]{:S(2)}) %all-to-all-start.1) | async-done | bytes 786464 | tf_op jit(solution)/shard_map/while/body/eval_jaxpr/all_to_all | solution.py:33
  348.6 16.7 %all_to_all.42 = bf16[16,16,1536]{2,1,0:T(8,128)(2,1)S(1)} all-to-all(bf16[16,16,1536]{2,1,0:T(8,128)(2,1)S(1)} %broadcast_in_dim.62), channel_id=1, replica_groups=mesh['section'=8,'rows'=16] {'rows'}, dimensions={0} | all-to-all | bytes 1572864 | tf_op jit(solution)/shard_map/while/body/eval_jaxpr/all_to_all | solution.py:18
  366.0 5.1 convolution_convert_fusion.2
  371.1 3.7 all-to-all-start.1
  375.5 12.2 %all-to-all-done.1 = bf16[16,16,1536]{2,1,0:T(8,128)(2,1)S(1)} async-done(((bf16[16,16,1536]{2,1,0:T(8,128)(2,1)}), bf16[16,16,1536]{2,1,0:T(8,128)(2,1)S(1)}, u32[]{:S(2)}, u32[]{:S(2)}) %all-to-all-start.1) | async-done | bytes 786464 | tf_op jit(solution)/shard_map/while/body/eval_jaxpr/all_to_all | solution.py:33
  396.1 16.7 %all_to_all.42 = bf16[16,16,1536]{2,1,0:T(8,128)(2,1)S(1)} all-to-all(bf16[16,16,1536]{2,1,0:T(8,128)(2,1)S(1)} %broadcast_in_dim.62), channel_id=1, replica_groups=mesh['section'=8,'rows'=16] {'rows'}, dimensions={0} | all-to-all | bytes 1572864 | tf_op jit(solution)/shard_map/while/body/eval_jaxpr/all_to_all | solution.py:18
  413.4 5.1 convolution_convert_fusion.2
  422.9 12.2 %all-to-all-done.1 = bf16[16,16,1536]{2,1,0:T(8,128)(2,1)S(1)} async-done(((bf16[16,16,1536]{2,1,0:T(8,128)(2,1)}), bf16[16,16,1536]{2,1,0:T(8,128)(2,1)S(1)}, u32[]{:S(2)}, u32[]{:S(2)}) %all-to-all-start.1) | async-done | bytes 786464 | tf_op jit(solution)/shard_map/while/body/eval_jaxpr/all_to_all | solution.py:33
  443.5 16.7 %all_to_all.42 = bf16[16,16,1536]{2,1,0:T(8,128)(2,1)S(1)} all-to-all(bf16[16,16,1536]{2,1,0:T(8,128)(2,1)S(1)} %broadcast_in_dim.62), channel_id=1, replica_groups=mesh['section'=8,'rows'=16] {'rows'}, dimensions={0} | all-to-all | bytes 1572864 | tf_op jit(solution)/shard_map/while/body/eval_jaxpr/all_to_all | solution.py:18
  460.9 5.1 convolution_convert_fusion.2
  470.4 12.2 %all-to-all-done.1 = bf16[16,16,1536]{2,1,0:T(8,128)(2,1)S(1)} async-done(((bf16[16,16,1536]{2,1,0:T(8,128)(2,1)}), bf16[16,16,1536]{2,1,0:T(8,128)(2,1)S(1)}, u32[]{:S(2)}, u32[]{:S(2)}) %all-to-all-start.1) | async-done | bytes 786464 | tf_op jit(solution)/shard_map/while/body/eval_jaxpr/all_to_all | solution.py:33
  491.0 16.7 %all_to_all.42 = bf16[16,16,1536]{2,1,0:T(8,128)(2,1)S(1)} all-to-all(bf16[16,16,1536]{2,1,0:T(8,128)(2,1)S(1)} %broadcast_in_dim.62), channel_id=1, replica_groups=mesh['section'=8,'rows'=16] {'rows'}, dimensions={0} | all-to-all | bytes 1572864 | tf_op jit(solution)/shard_map/while/body/eval_jaxpr/all_to_all | solution.py:18
  508.4 5.1 convolution_convert_fusion.2
  517.9 12.2 %all-to-all-done.1 = bf16[16,16,1536]{2,1,0:T(8,128)(2,1)S(1)} async-done(((bf16[16,16,1536]{2,1,0:T(8,128)(2,1)}), bf16[16,16,1536]{2,1,0:T(8,128)(2,1)S(1)}, u32[]{:S(2)}, u32[]{:S(2)}) %all-to-all-start.1) | async-done | bytes 786464 | tf_op jit(solution)/shard_map/while/body/eval_jaxpr/all_to_all | solution.py:33
  538.5 16.7 %all_to_all.42 = bf16[16,16,1536]{2,1,0:T(8,128)(2,1)S(1)} all-to-all(bf16[16,16,1536]{2,1,0:T(8,128)(2,1)S(1)} %broadcast_in_dim.62), channel_id=1, replica_groups=mesh['section'=8,'rows'=16] {'rows'}, dimensions={0} | all-to-all | bytes 1572864 | tf_op jit(solution)/shard_map/while/body/eval_jaxpr/all_to_all | solution.py:18
  555.9 5.1 convolution_convert_fusion.2
  561.0 3.7 all-to-all-start.1
  565.4 12.2 %all-to-all-done.1 = bf16[16,16,1536]{2,1,0:T(8,128)(2,1)S(1)} async-done(((bf16[16,16,1536]{2,1,0:T(8,128)(2,1)}), bf16[16,16,1536]{2,1,0:T(8,128)(2,1)S(1)}, u32[]{:S(2)}, u32[]{:S(2)}) %all-to-all-start.1) | async-done | bytes 786464 | tf_op jit(solution)/shard_map/while/body/eval_jaxpr/all_to_all | solution.py:33
  586.0 16.7 %all_to_all.42 = bf16[16,16,1536]{2,1,0:T(8,128)(2,1)S(1)} all-to-all(bf16[16,16,1536]{2,1,0:T(8,128)(2,1)S(1)} %broadcast_in_dim.62), channel_id=1, replica_groups=mesh['section'=8,'rows'=16] {'rows'}, dimensions={0} | all-to-all | bytes 1572864 | tf_op jit(solution)/shard_map/while/body/eval_jaxpr/all_to_all | solution.py:18
  603.3 5.1 convolution_convert_fusion.2
  612.8 12.2 %all-to-all-done.1 = bf16[16,16,1536]{2,1,0:T(8,128)(2,1)S(1)} async-done(((bf16[16,16,1536]{2,1,0:T(8,128)(2,1)}), bf16[16,16,1536]{2,1,0:T(8,128)(2,1)S(1)}, u32[]{:S(2)}, u32[]{:S(2)}) %all-to-all-start.1) | async-done | bytes 786464 | tf_op jit(solution)/shard_map/while/body/eval_jaxpr/all_to_all | solution.py:33
  633.4 16.8 %all_to_all.42 = bf16[16,16,1536]{2,1,0:T(8,128)(2,1)S(1)} all-to-all(bf16[16,16,1536]{2,1,0:T(8,128)(2,1)S(1)} %broadcast_in_dim.62), channel_id=1, replica_groups=mesh['section'=8,'rows'=16] {'rows'}, dimensions={0} | all-to-all | bytes 1572864 | tf_op jit(solution)/shard_map/while/body/eval_jaxpr/all_to_all | solution.py:18
  650.8 5.1 convolution_convert_fusion.2
  655.9 3.7 all-to-all-start.1
  660.3 12.2 %all-to-all-done.1 = bf16[16,16,1536]{2,1,0:T(8,128)(2,1)S(1)} async-done(((bf16[16,16,1536]{2,1,0:T(8,128)(2,1)}), bf16[16,16,1536]{2,1,0:T(8,128)(2,1)S(1)}, u32[]{:S(2)}, u32[]{:S(2)}) %all-to-all-start.1) | async-done | bytes 786464 | tf_op jit(solution)/shard_map/while/body/eval_jaxpr/all_to_all | solution.py:33
  680.9 16.7 %all_to_all.42 = bf16[16,16,1536]{2,1,0:T(8,128)(2,1)S(1)} all-to-all(bf16[16,16,1536]{2,1,0:T(8,128)(2,1)S(1)} %broadcast_in_dim.62), channel_id=1, replica_groups=mesh['section'=8,'rows'=16] {'rows'}, dimensions={0} | all-to-all | bytes 1572864 | tf_op jit(solution)/shard_map/while/body/eval_jaxpr/all_to_all | solution.py:18
  698.3 5.1 convolution_convert_fusion.2
  703.4 3.7 all-to-all-start.1
  707.8 12.2 %all-to-all-done.1 = bf16[16,16,1536]{2,1,0:T(8,128)(2,1)S(1)} async-done(((bf16[16,16,1536]{2,1,0:T(8,128)(2,1)}), bf16[16,16,1536]{2,1,0:T(8,128)(2,1)S(1)}, u32[]{:S(2)}, u32[]{:S(2)}) %all-to-all-start.1) | async-done | bytes 786464 | tf_op jit(solution)/shard_map/while/body/eval_jaxpr/all_to_all | solution.py:33
  728.4 9.0 %all-gather.1 = f32[8,1,128]{2,1,0:T(1,128)S(1)} all-gather(f32[1,1,128]{2,1,0:T(1,128)S(1)} %bitcast.69), channel_id=2, replica_groups=mesh['section'=8,'rows'=16] {'section'}, dimensions={0}, use_global_device_ids=true | all-gather | bytes 4608 | tf_op jit(solution)/shard_map/all_gather | solution.py:44
  739.6 4.2 all-to-all-start.3
  745.5 4.7 all-to-all-done.3
  755.5 4.4 all-to-all-done.2
  767.3 6.4 all-to-all-done.4
  (303 shorter events, 154.7 us)
Async XLA Ops:
  3.6 723.6 %copy-start.5 = (f32[1536]{0:T(1024)S(1)}, f32[1536]{0:T(1024)}, u32[]{:S(2)}) copy-start(f32[1536]{0:T(1024)} %param.26) | copy-start | bytes 18436
  3.6 723.6 %copy-start.6 = (f32[1536]{0:T(1024)S(1)}, f32[1536]{0:T(1024)}, u32[]{:S(2)}) copy-start(f32[1536]{0:T(1024)} %param.25) | copy-start | bytes 18436
  3.6 733.8 %copy-start.7 = (s32[128,1]{0,1:T(1,128)S(1)}, s32[128,1]{0,1:T(1,128)}, u32[]{:S(2)}) copy-start(s32[128,1]{0,1:T(1,128)} %param.19) | copy-start | bytes 1540
  3.6 734.3 %copy-start.8 = (f32[128]{0:T(128)S(1)}, f32[128]{0:T(128)}, u32[]{:S(2)}) copy-start(f32[128]{0:T(128)} %param.18) | copy-start | bytes 1540
  3.6 740.2 %copy-start.9 = (s32[128]{0:T(128)S(1)}, s32[128]{0:T(128)}, u32[]{:S(2)}) copy-start(s32[128]{0:T(128)} %param.20) | copy-start | bytes 1540
  3.6 758.3 %copy-start.4 = (f32[4096]{0:T(1024)S(1)}, f32[4096]{0:T(1024)}, u32[]{:S(2)}) copy-start(f32[4096]{0:T(1024)} %param.27) | copy-start | bytes 49156
  3.7 23.3 %copy-start.1 = (bf16[1,1536,560]{1,2,0:T(8,128)(2,1)S(1)}, bf16[1,1536,560]{1,2,0:T(8,128)(2,1)}, u32[]{:S(2)}) copy-start(bf16[1,1536,560]{1,2,0:T(8,128)(2,1)} %get-tuple-element.283) | copy-start | bytes 5160964 | tf_op jit(solution)/shard_map/while
  32.7 25.2 %copy-start.3 = (bf16[128,1536]{1,0:T(8,128)(2,1)S(1)}, bf16[128,1536]{1,0:T(8,128)(2,1)}, u32[]{:S(2)}) copy-start(bf16[128,1536]{1,0:T(8,128)(2,1)} %copy-done.2) | copy-start | bytes 1179652 | tf_op jit(solution)/shard_map/while
  32.7 16.4 %all-to-all-start.1 = ((bf16[16,16,1536]{2,1,0:T(8,128)(2,1)}), bf16[16,16,1536]{2,1,0:T(8,128)(2,1)S(1)}, u32[]{:S(2)}, u32[]{:S(2)}) async-start(bf16[16,16,1536]{2,1,0:T(8,128)(2,1)} %bitcast.64), calls=%async_computation.1 | async-start | bytes 1572864 | tf_op jit(solution)/shard_map/while/body/eval_jaxpr/all_to_all | solution.py:33
  50.7 7.2 collective-permute-start
  81.8 25.7 %copy-start.3 = (bf16[128,1536]{1,0:T(8,128)(2,1)S(1)}, bf16[128,1536]{1,0:T(8,128)(2,1)}, u32[]{:S(2)}) copy-start(bf16[128,1536]{1,0:T(8,128)(2,1)} %copy-done.2) | copy-start | bytes 1179652 | tf_op jit(solution)/shard_map/while
  81.8 19.2 %all-to-all-start.1 = ((bf16[16,16,1536]{2,1,0:T(8,128)(2,1)}), bf16[16,16,1536]{2,1,0:T(8,128)(2,1)S(1)}, u32[]{:S(2)}, u32[]{:S(2)}) async-start(bf16[16,16,1536]{2,1,0:T(8,128)(2,1)} %bitcast.64), calls=%async_computation.1 | async-start | bytes 1572864 | tf_op jit(solution)/shard_map/while/body/eval_jaxpr/all_to_all | solution.py:33
  102.6 4.9 collective-permute-start
  131.8 24.5 %copy-start.3 = (bf16[128,1536]{1,0:T(8,128)(2,1)S(1)}, bf16[128,1536]{1,0:T(8,128)(2,1)}, u32[]{:S(2)}) copy-start(bf16[128,1536]{1,0:T(8,128)(2,1)} %copy-done.2) | copy-start | bytes 1179652 | tf_op jit(solution)/shard_map/while
  131.9 19.8 %all-to-all-start.1 = ((bf16[16,16,1536]{2,1,0:T(8,128)(2,1)}), bf16[16,16,1536]{2,1,0:T(8,128)(2,1)S(1)}, u32[]{:S(2)}, u32[]{:S(2)}) async-start(bf16[16,16,1536]{2,1,0:T(8,128)(2,1)} %bitcast.64), calls=%async_computation.1 | async-start | bytes 1572864 | tf_op jit(solution)/shard_map/while/body/eval_jaxpr/all_to_all | solution.py:33
  153.2 3.1 collective-permute-start
  156.3 19.1 %copy-start.1 = (bf16[1,1536,560]{1,2,0:T(8,128)(2,1)S(1)}, bf16[1,1536,560]{1,2,0:T(8,128)(2,1)}, u32[]{:S(2)}) copy-start(bf16[1,1536,560]{1,2,0:T(8,128)(2,1)} %get-tuple-element.283) | copy-start | bytes 5160964 | tf_op jit(solution)/shard_map/while
  181.2 22.7 %copy-start.3 = (bf16[128,1536]{1,0:T(8,128)(2,1)S(1)}, bf16[128,1536]{1,0:T(8,128)(2,1)}, u32[]{:S(2)}) copy-start(bf16[128,1536]{1,0:T(8,128)(2,1)} %copy-done.2) | copy-start | bytes 1179652 | tf_op jit(solution)/shard_map/while
  181.2 16.7 %all-to-all-start.1 = ((bf16[16,16,1536]{2,1,0:T(8,128)(2,1)}), bf16[16,16,1536]{2,1,0:T(8,128)(2,1)S(1)}, u32[]{:S(2)}, u32[]{:S(2)}) async-start(bf16[16,16,1536]{2,1,0:T(8,128)(2,1)} %bitcast.64), calls=%async_computation.1 | async-start | bytes 1572864 | tf_op jit(solution)/shard_map/while/body/eval_jaxpr/all_to_all | solution.py:33
  199.5 4.4 collective-permute-start
  228.6 22.6 %copy-start.3 = (bf16[128,1536]{1,0:T(8,128)(2,1)S(1)}, bf16[128,1536]{1,0:T(8,128)(2,1)}, u32[]{:S(2)}) copy-start(bf16[128,1536]{1,0:T(8,128)(2,1)} %copy-done.2) | copy-start | bytes 1179652 | tf_op jit(solution)/shard_map/while
  228.6 16.6 %all-to-all-start.1 = ((bf16[16,16,1536]{2,1,0:T(8,128)(2,1)}), bf16[16,16,1536]{2,1,0:T(8,128)(2,1)S(1)}, u32[]{:S(2)}, u32[]{:S(2)}) async-start(bf16[16,16,1536]{2,1,0:T(8,128)(2,1)} %bitcast.64), calls=%async_computation.1 | async-start | bytes 1572864 | tf_op jit(solution)/shard_map/while/body/eval_jaxpr/all_to_all | solution.py:33
  246.8 4.4 collective-permute-start
  251.2 19.1 %copy-start.1 = (bf16[1,1536,560]{1,2,0:T(8,128)(2,1)S(1)}, bf16[1,1536,560]{1,2,0:T(8,128)(2,1)}, u32[]{:S(2)}) copy-start(bf16[1,1536,560]{1,2,0:T(8,128)(2,1)} %get-tuple-element.283) | copy-start | bytes 5160964 | tf_op jit(solution)/shard_map/while
  276.1 22.6 %copy-start.3 = (bf16[128,1536]{1,0:T(8,128)(2,1)S(1)}, bf16[128,1536]{1,0:T(8,128)(2,1)}, u32[]{:S(2)}) copy-start(bf16[128,1536]{1,0:T(8,128)(2,1)} %copy-done.2) | copy-start | bytes 1179652 | tf_op jit(solution)/shard_map/while
  276.1 16.6 %all-to-all-start.1 = ((bf16[16,16,1536]{2,1,0:T(8,128)(2,1)}), bf16[16,16,1536]{2,1,0:T(8,128)(2,1)S(1)}, u32[]{:S(2)}, u32[]{:S(2)}) async-start(bf16[16,16,1536]{2,1,0:T(8,128)(2,1)} %bitcast.64), calls=%async_computation.1 | async-start | bytes 1572864 | tf_op jit(solution)/shard_map/while/body/eval_jaxpr/all_to_all | solution.py:33
  294.3 4.4 collective-permute-start
  298.7 19.1 %copy-start.1 = (bf16[1,1536,560]{1,2,0:T(8,128)(2,1)S(1)}, bf16[1,1536,560]{1,2,0:T(8,128)(2,1)}, u32[]{:S(2)}) copy-start(bf16[1,1536,560]{1,2,0:T(8,128)(2,1)} %get-tuple-element.283) | copy-start | bytes 5160964 | tf_op jit(solution)/shard_map/while
  323.6 22.6 %copy-start.3 = (bf16[128,1536]{1,0:T(8,128)(2,1)S(1)}, bf16[128,1536]{1,0:T(8,128)(2,1)}, u32[]{:S(2)}) copy-start(bf16[128,1536]{1,0:T(8,128)(2,1)} %copy-done.2) | copy-start | bytes 1179652 | tf_op jit(solution)/shard_map/while
  323.6 16.6 %all-to-all-start.1 = ((bf16[16,16,1536]{2,1,0:T(8,128)(2,1)}), bf16[16,16,1536]{2,1,0:T(8,128)(2,1)S(1)}, u32[]{:S(2)}, u32[]{:S(2)}) async-start(bf16[16,16,1536]{2,1,0:T(8,128)(2,1)} %bitcast.64), calls=%async_computation.1 | async-start | bytes 1572864 | tf_op jit(solution)/shard_map/while/body/eval_jaxpr/all_to_all | solution.py:33
  341.7 4.4 collective-permute-start
  346.2 19.1 %copy-start.1 = (bf16[1,1536,560]{1,2,0:T(8,128)(2,1)S(1)}, bf16[1,1536,560]{1,2,0:T(8,128)(2,1)}, u32[]{:S(2)}) copy-start(bf16[1,1536,560]{1,2,0:T(8,128)(2,1)} %get-tuple-element.283) | copy-start | bytes 5160964 | tf_op jit(solution)/shard_map/while
  371.1 22.6 %copy-start.3 = (bf16[128,1536]{1,0:T(8,128)(2,1)S(1)}, bf16[128,1536]{1,0:T(8,128)(2,1)}, u32[]{:S(2)}) copy-start(bf16[128,1536]{1,0:T(8,128)(2,1)} %copy-done.2) | copy-start | bytes 1179652 | tf_op jit(solution)/shard_map/while
  371.1 16.6 %all-to-all-start.1 = ((bf16[16,16,1536]{2,1,0:T(8,128)(2,1)}), bf16[16,16,1536]{2,1,0:T(8,128)(2,1)S(1)}, u32[]{:S(2)}, u32[]{:S(2)}) async-start(bf16[16,16,1536]{2,1,0:T(8,128)(2,1)} %bitcast.64), calls=%async_computation.1 | async-start | bytes 1572864 | tf_op jit(solution)/shard_map/while/body/eval_jaxpr/all_to_all | solution.py:33
  389.2 4.4 collective-permute-start
  393.7 19.1 %copy-start.1 = (bf16[1,1536,560]{1,2,0:T(8,128)(2,1)S(1)}, bf16[1,1536,560]{1,2,0:T(8,128)(2,1)}, u32[]{:S(2)}) copy-start(bf16[1,1536,560]{1,2,0:T(8,128)(2,1)} %get-tuple-element.283) | copy-start | bytes 5160964 | tf_op jit(solution)/shard_map/while
  418.5 22.6 %copy-start.3 = (bf16[128,1536]{1,0:T(8,128)(2,1)S(1)}, bf16[128,1536]{1,0:T(8,128)(2,1)}, u32[]{:S(2)}) copy-start(bf16[128,1536]{1,0:T(8,128)(2,1)} %copy-done.2) | copy-start | bytes 1179652 | tf_op jit(solution)/shard_map/while
  418.5 16.6 %all-to-all-start.1 = ((bf16[16,16,1536]{2,1,0:T(8,128)(2,1)}), bf16[16,16,1536]{2,1,0:T(8,128)(2,1)S(1)}, u32[]{:S(2)}, u32[]{:S(2)}) async-start(bf16[16,16,1536]{2,1,0:T(8,128)(2,1)} %bitcast.64), calls=%async_computation.1 | async-start | bytes 1572864 | tf_op jit(solution)/shard_map/while/body/eval_jaxpr/all_to_all | solution.py:33
  436.7 4.4 collective-permute-start
  441.2 19.1 %copy-start.1 = (bf16[1,1536,560]{1,2,0:T(8,128)(2,1)S(1)}, bf16[1,1536,560]{1,2,0:T(8,128)(2,1)}, u32[]{:S(2)}) copy-start(bf16[1,1536,560]{1,2,0:T(8,128)(2,1)} %get-tuple-element.283) | copy-start | bytes 5160964 | tf_op jit(solution)/shard_map/while
  466.0 22.6 %copy-start.3 = (bf16[128,1536]{1,0:T(8,128)(2,1)S(1)}, bf16[128,1536]{1,0:T(8,128)(2,1)}, u32[]{:S(2)}) copy-start(bf16[128,1536]{1,0:T(8,128)(2,1)} %copy-done.2) | copy-start | bytes 1179652 | tf_op jit(solution)/shard_map/while
  466.0 16.6 %all-to-all-start.1 = ((bf16[16,16,1536]{2,1,0:T(8,128)(2,1)}), bf16[16,16,1536]{2,1,0:T(8,128)(2,1)S(1)}, u32[]{:S(2)}, u32[]{:S(2)}) async-start(bf16[16,16,1536]{2,1,0:T(8,128)(2,1)} %bitcast.64), calls=%async_computation.1 | async-start | bytes 1572864 | tf_op jit(solution)/shard_map/while/body/eval_jaxpr/all_to_all | solution.py:33
  484.2 4.4 collective-permute-start
  513.5 22.6 %copy-start.3 = (bf16[128,1536]{1,0:T(8,128)(2,1)S(1)}, bf16[128,1536]{1,0:T(8,128)(2,1)}, u32[]{:S(2)}) copy-start(bf16[128,1536]{1,0:T(8,128)(2,1)} %copy-done.2) | copy-start | bytes 1179652 | tf_op jit(solution)/shard_map/while
  513.5 16.6 %all-to-all-start.1 = ((bf16[16,16,1536]{2,1,0:T(8,128)(2,1)}), bf16[16,16,1536]{2,1,0:T(8,128)(2,1)S(1)}, u32[]{:S(2)}, u32[]{:S(2)}) async-start(bf16[16,16,1536]{2,1,0:T(8,128)(2,1)} %bitcast.64), calls=%async_computation.1 | async-start | bytes 1572864 | tf_op jit(solution)/shard_map/while/body/eval_jaxpr/all_to_all | solution.py:33
  531.7 4.4 collective-permute-start
  536.1 19.1 %copy-start.1 = (bf16[1,1536,560]{1,2,0:T(8,128)(2,1)S(1)}, bf16[1,1536,560]{1,2,0:T(8,128)(2,1)}, u32[]{:S(2)}) copy-start(bf16[1,1536,560]{1,2,0:T(8,128)(2,1)} %get-tuple-element.283) | copy-start | bytes 5160964 | tf_op jit(solution)/shard_map/while
  561.0 22.6 %copy-start.3 = (bf16[128,1536]{1,0:T(8,128)(2,1)S(1)}, bf16[128,1536]{1,0:T(8,128)(2,1)}, u32[]{:S(2)}) copy-start(bf16[128,1536]{1,0:T(8,128)(2,1)} %copy-done.2) | copy-start | bytes 1179652 | tf_op jit(solution)/shard_map/while
  561.0 16.6 %all-to-all-start.1 = ((bf16[16,16,1536]{2,1,0:T(8,128)(2,1)}), bf16[16,16,1536]{2,1,0:T(8,128)(2,1)S(1)}, u32[]{:S(2)}, u32[]{:S(2)}) async-start(bf16[16,16,1536]{2,1,0:T(8,128)(2,1)} %bitcast.64), calls=%async_computation.1 | async-start | bytes 1572864 | tf_op jit(solution)/shard_map/while/body/eval_jaxpr/all_to_all | solution.py:33
  579.1 4.4 collective-permute-start
  583.6 19.1 %copy-start.1 = (bf16[1,1536,560]{1,2,0:T(8,128)(2,1)S(1)}, bf16[1,1536,560]{1,2,0:T(8,128)(2,1)}, u32[]{:S(2)}) copy-start(bf16[1,1536,560]{1,2,0:T(8,128)(2,1)} %get-tuple-element.283) | copy-start | bytes 5160964 | tf_op jit(solution)/shard_map/while
  608.4 22.6 %copy-start.3 = (bf16[128,1536]{1,0:T(8,128)(2,1)S(1)}, bf16[128,1536]{1,0:T(8,128)(2,1)}, u32[]{:S(2)}) copy-start(bf16[128,1536]{1,0:T(8,128)(2,1)} %copy-done.2) | copy-start | bytes 1179652 | tf_op jit(solution)/shard_map/while
  608.4 16.6 %all-to-all-start.1 = ((bf16[16,16,1536]{2,1,0:T(8,128)(2,1)}), bf16[16,16,1536]{2,1,0:T(8,128)(2,1)S(1)}, u32[]{:S(2)}, u32[]{:S(2)}) async-start(bf16[16,16,1536]{2,1,0:T(8,128)(2,1)} %bitcast.64), calls=%async_computation.1 | async-start | bytes 1572864 | tf_op jit(solution)/shard_map/while/body/eval_jaxpr/all_to_all | solution.py:33
  626.6 4.5 collective-permute-start
  631.0 19.1 %copy-start.1 = (bf16[1,1536,560]{1,2,0:T(8,128)(2,1)S(1)}, bf16[1,1536,560]{1,2,0:T(8,128)(2,1)}, u32[]{:S(2)}) copy-start(bf16[1,1536,560]{1,2,0:T(8,128)(2,1)} %get-tuple-element.283) | copy-start | bytes 5160964 | tf_op jit(solution)/shard_map/while
  655.9 22.6 %copy-start.3 = (bf16[128,1536]{1,0:T(8,128)(2,1)S(1)}, bf16[128,1536]{1,0:T(8,128)(2,1)}, u32[]{:S(2)}) copy-start(bf16[128,1536]{1,0:T(8,128)(2,1)} %copy-done.2) | copy-start | bytes 1179652 | tf_op jit(solution)/shard_map/while
  655.9 16.6 %all-to-all-start.1 = ((bf16[16,16,1536]{2,1,0:T(8,128)(2,1)}), bf16[16,16,1536]{2,1,0:T(8,128)(2,1)S(1)}, u32[]{:S(2)}, u32[]{:S(2)}) async-start(bf16[16,16,1536]{2,1,0:T(8,128)(2,1)} %bitcast.64), calls=%async_computation.1 | async-start | bytes 1572864 | tf_op jit(solution)/shard_map/while/body/eval_jaxpr/all_to_all | solution.py:33
  674.1 4.4 collective-permute-start
  703.4 22.6 %copy-start.3 = (bf16[128,1536]{1,0:T(8,128)(2,1)S(1)}, bf16[128,1536]{1,0:T(8,128)(2,1)}, u32[]{:S(2)}) copy-start(bf16[128,1536]{1,0:T(8,128)(2,1)} %copy-done.2) | copy-start | bytes 1179652 | tf_op jit(solution)/shard_map/while
  703.4 16.6 %all-to-all-start.1 = ((bf16[16,16,1536]{2,1,0:T(8,128)(2,1)}), bf16[16,16,1536]{2,1,0:T(8,128)(2,1)S(1)}, u32[]{:S(2)}, u32[]{:S(2)}) async-start(bf16[16,16,1536]{2,1,0:T(8,128)(2,1)} %bitcast.64), calls=%async_computation.1 | async-start | bytes 1572864 | tf_op jit(solution)/shard_map/while/body/eval_jaxpr/all_to_all | solution.py:33
  721.5 4.5 collective-permute-start
  739.6 10.6 %all-to-all-start.3 = ((f32[16,32,1]{1,2,0:T(1,128)}), f32[16,32,1]{1,2,0:T(1,128)S(1)}, u32[]{:S(2)}, u32[]{:S(2)}) async-start(f32[16,32,1]{1,2,0:T(1,128)} %bitcast.15), calls=%async_computation.3 | async-start | bytes 16384 | tf_op jit(solution)/shard_map/all_to_all | solution.py:132
  750.2 9.6 %all-to-all-start.2 = ((f32[16,32,1]{1,2,0:T(1,128)}), f32[16,32,1]{1,2,0:T(1,128)S(1)}, u32[]{:S(2)}, u32[]{:S(2)}) async-start(f32[16,32,1]{1,2,0:T(1,128)} %bitcast.13), calls=%async_computation.2 | async-start | bytes 16384 | tf_op jit(solution)/shard_map/all_to_all | solution.py:133
  763.8 9.9 %all-to-all-start.4 = ((f32[16,1,1]{2,1,0:T(1,128)}), f32[16,1,1]{2,1,0:T(1,128)S(1)}, u32[]{:S(2)}, u32[]{:S(2)}) async-start(f32[16,1,1]{2,1,0:T(1,128)} %broadcast_in_dim.54), calls=%async_computation.4 | async-start | bytes 16384 | tf_op jit(solution)/shard_map/all_to_all | solution.py:18
  (21 other events, 129.1 us)
where the time goes:
time: 783 us; the launch traced here: 776 us
  blocking collectives  263 us (34%)
  waiting for transfers between devices  238 us (30%)
  starting transfers between devices  102 us (13%)
  matrix products  87.4 us (11%)
  other arithmetic  44.9 us (6%)
  loops' own time  20.8 us (3%)
  local copies, waits for them, and re-layouts  18.4 us (2%)
    all_to_all x15, blocking collectives, from_everyone(): return lax.all_to_all(copies, axis, split_axis=0, concat_axis=0, tiled=True)  254 us
    all_to_all x15, waiting for transfers between devices, summed_on_arrival(): parts = lax.all_to_all(cut_along(shard, dim, count), axis, 0, 0, tiled=True)  189 us
    dot_general x15, matrix products, layer_split(): jnp.dot(hidden, w_down[layer], preferred_element_type=jnp.float32)  76.5 us
    all_to_all x15, starting transfers between devices, summed_on_arrival(): parts = lax.all_to_all(cut_along(shard, dim, count), axis, 0, 0, tiled=True)  56.2 us
    ppermute x15, starting transfers between devices, shifted(): lax.ppermute(value, axis, [(source, source + steps) for source in range(f...  34.6 us
    ppermute x15, waiting for transfers between devices, shifted(): lax.ppermute(value, axis, [(source, source + steps) for source in range(f...  33.7 us
    select_n x15, other arithmetic, tick(): collected = jnp.where(valid, placed, collected)  21.6 us
    another operation x1, loops' own time, on_device(): lax.scan(tick, (start_state, start_rows), jnp.arange(MICRO + sections - 1))  20.8 us
  transfers between devices with their start and end apart: 33, of which 33 were waited for; matrix products, arithmetic and copies ran while one was open for 0% of the time, Pallas kernels for 0%

commit v1 on v0

v1 whole, which is shorter than its diff:
```python
import functools

import jax
import jax.numpy as jnp
from jax import lax
from jax.experimental import pallas as pl
from jax.experimental.pallas import tpu as pltpu
from jax.sharding import PartitionSpec as P

MESH = pl.DeviceIdType.MESH
MICRO = 16
GROUP = 8
SPAN = 640


def place(member, half):
    y = member // 2
    return 4 * y + 2 * (member % 2) + (y + half) % 2


def copy_to(src, dst, send, recv, section, rows):
    return pltpu.make_async_remote_copy(
        src_ref=src,
        dst_ref=dst,
        send_sem=send,
        recv_sem=recv,
        device_id={"section": section, "rows": rows},
        device_id_type=MESH,
    )


def take(ref, sem):
    pltpu.make_async_copy(ref, ref, sem).wait()


def model_kernel(
    x0,
    gain_in,
    wg_in,
    wu_in,
    wd_in,
    final_gain,
    head,
    out,
    wg,
    wu,
    wd,
    gain,
    xs,
    ag,
    rs,
    ps,
    hid,
    rew,
    news,
    allrew,
    own_sem,
    w0_send,
    w0_recv,
    w1_send,
    w1_recv,
    x_send,
    x_recv,
    ag_send,
    ag_recv,
    rs_send,
    rs_recv,
    all_send,
    all_recv,
):
    section = lax.axis_index("section")
    rows = lax.axis_index("rows")
    plane, core = section // 2, section % 2
    y, x = rows // 4, rows % 4
    half = (x + y) % 2
    stage = 2 * plane + half
    member = y * 2 + x // 2
    primary = core == half
    sibling = 2 * plane + 1 - core
    later = (stage + 1) % 8
    later_half = later % 2
    later_section = 2 * (later // 2) + core
    width = x0.shape[-1]
    r = x0.shape[1]
    block = GROUP * r

    near = (
        4 * y + (x + 1) % 4,
        4 * y + (x + 3) % 4,
        4 * ((y + 1) % 4) + x,
        4 * ((y + 3) % 4) + x,
    )
    lanes = ((0, 128), (128, 128), (256, 128), (384, 256))
    downs = ((0, 128), (128, 128), (256, 128), (384, 176))

    def own_copies():
        return (
            pltpu.make_async_copy(wg_in, wg.at[:, pl.ds(0, SPAN)], own_sem.at[0]),
            pltpu.make_async_copy(wu_in, wu.at[:, pl.ds(0, SPAN)], own_sem.at[1]),
            pltpu.make_async_copy(wd_in, wd.at[pl.ds(0, SPAN), :], own_sem.at[2]),
            pltpu.make_async_copy(gain_in, gain, own_sem.at[3]),
        )

    def sibling_copies():
        pairs = (
            (wg_in, wg.at[:, pl.ds(0, SPAN)]),
            (wu_in, wu.at[:, pl.ds(0, SPAN)]),
            (wd_in, wd.at[pl.ds(0, SPAN), :]),
            (gain_in, gain),
        )
        return [
            copy_to(src, dst, w0_send.at[i], w0_recv.at[i], sibling, rows)
            for i, (src, dst) in enumerate(pairs)
        ]

    def piece_copies(n, to_section, to_rows, relay):
        at, size = lanes[n]
        d_at, d_size = downs[n]
        g_dst = wg.at[:, pl.ds(SPAN + at, size)]
        u_dst = wu.at[:, pl.ds(SPAN + at, size)]
        d_dst = wd.at[pl.ds(SPAN + d_at, d_size), :]
        sources = (
            (g_dst, u_dst, d_dst)
            if relay
            else (
                wg_in.at[:, pl.ds(at, size)],
                wu_in.at[:, pl.ds(at, size)],
                wd_in.at[pl.ds(d_at, d_size), :],
            )
        )
        return [
            copy_to(src, dst, w1_send.at[i, n], w1_recv.at[i, n], to_section, to_rows)
            for i, (src, dst) in enumerate(zip(sources, (g_dst, u_dst, d_dst)))
        ]

    @pl.when(primary)
    def _():
        for copy in own_copies():
            copy.start()
        for copy in sibling_copies():
            copy.start()

    @pl.when(jnp.logical_not(primary))
    def _():
        for n in range(4):
            for copy in piece_copies(n, section, near[n], False):
                copy.start()

    wd[pl.ds(SPAN + 560, SPAN - 560), :] = jnp.zeros((SPAN - 560, width), jnp.bfloat16)

    def feed():
        return copy_to(x0, xs, x_send, x_recv, section, place(member, 0))

    @pl.when(jnp.logical_and(section == 1, half == 1))
    def _():
        feed().start()

    @pl.when(jnp.logical_and(section == 0, half == 0))
    def _():
        xs[...] = x0[...]

    def summed(m):
        take(rs.at[m], rs_recv.at[m])
        total = rs[m, 0].astype(jnp.float32)
        for i in range(1, GROUP + 1):
            total = total + rs[m, i].astype(jnp.float32)
        return total.astype(jnp.bfloat16)

    def enter(m):
        @pl.when(stage > 0)
        def _():
            xs[m] = summed(m)

        copy_to(
            xs.at[m],
            rs.at[m, GROUP],
            rs_send.at[m],
            rs_recv.at[m],
            later_section,
            place(member, later_half),
        ).start()
        wide = xs[m].astype(jnp.float32)
        mean = jnp.mean(wide * wide, axis=-1, keepdims=True)
        ag[m, member] = (wide * lax.rsqrt(mean + 1e-06) * gain[...]).astype(jnp.bfloat16)
        for step in range(1, GROUP):
            peer = (member + step) % GROUP
            copy_to(
                ag.at[m, member],
                ag.at[m, member],
                ag_send.at[m],
                ag_recv.at[m],
                section,
                place(peer, half),
            ).start()

    def layer(m):
        take(ag.at[m, pl.ds(0, GROUP - 1)], ag_recv.at[m])
        normed = ag[m].reshape(block, width)
        for at in range(0, 2 * SPAN, 256):
            gate = jnp.dot(normed, wg[:, at : at + 256], preferred_element_type=jnp.float32)
            upper = jnp.dot(normed, wu[:, at : at + 256], preferred_element_type=jnp.float32)
            hid[:, at : at + 256] = (gate * jax.nn.sigmoid(gate) * upper).astype(jnp.bfloat16)
        for at in range(0, width, 256):
            part = jnp.dot(hid[...], wd[:, at : at + 256], preferred_element_type=jnp.float32)
            ps[m, :, :, at : at + 256] = part.astype(jnp.bfloat16).reshape(GROUP, r, 256)
        for step in range(GROUP):
            peer = (member + step) % GROUP
            copy_to(
                ps.at[m, peer],
                rs.at[m, member],
                rs_send.at[m],
                rs_recv.at[m],
                later_section,
                place(peer, later_half),
            ).start()

    @pl.when(jnp.logical_and(section == 1, half == 0))
    def _():
        take(xs, x_recv)

    @pl.when(primary)
    def _():
        own_copies()[3].wait()

    @pl.when(jnp.logical_not(primary))
    def _():
        take(gain, w0_recv.at[3])

    @pl.when(stage == 0)
    def _():
        enter(0)

    @pl.when(primary)
    def _():
        for n in range(4):
            for i, copy in enumerate(piece_copies(n, sibling, rows, True)):
                copy.wait_recv()
                copy.start()
        for copy in own_copies()[:3]:
            copy.wait()

    @pl.when(jnp.logical_not(primary))
    def _():
        for copy in sibling_copies()[:3]:
            copy.wait_recv()
        for n in range(4):
            for copy in piece_copies(n, section, near[n], False):
                copy.wait_recv()

    @pl.when(stage > 0)
    def _():
        enter(0)

    def tick(m, carry):
        @pl.when(m + 1 < MICRO)
        def _():
            enter(m + 1)

        layer(m)
        return carry

    lax.fori_loop(0, MICRO, tick, 0)

    def reach(step):
        flat = (section * 16 + rows + step) % 128
        return copy_to(
            news,
            allrew.at[place(member, core)],
            all_send,
            all_recv,
            flat // 16,
            flat % 16,
        )

    @pl.when(stage == 0)
    def _():
        def finish(m, line):
            wide = summed(m).astype(jnp.float32)
            mean = jnp.mean(wide * wide, axis=-1, keepdims=True)
            ready = wide * lax.rsqrt(mean + 1e-06) * final_gain[...]
            value = jnp.sum(ready * head[...], axis=-1, keepdims=True)
            spot = lax.broadcasted_iota(jnp.int32, (r, 128), 0) + m * r
            lane = lax.broadcasted_iota(jnp.int32, (r, 128), 1)
            return line + jnp.where(spot == lane, value, 0.0)

        line = lax.fori_loop(0, MICRO, finish, jnp.zeros((r, 128), jnp.float32))
        line = jnp.broadcast_to(jnp.sum(line, axis=0, keepdims=True), (8, 128))
        news[...] = line
        allrew[place(member, core)] = line

        def send(step, carry):
            reach(step).start()
            return carry

        lax.fori_loop(1, 128, send, 0)
        take(allrew.at[pl.ds(0, 15)], all_recv)

    @pl.when(stage > 0)
    def _():
        take(allrew, all_recv)

    out[...] = allrew[...]

    @pl.when(stage == 0)
    def _():
        def sent(step, carry):
            take(allrew, all_send)
            return carry

        lax.fori_loop(0, 7, sent, 0)
        take(allrew.at[pl.ds(0, 15)], all_send)

    def drained(m, carry):
        take(ag.at[m, pl.ds(0, GROUP - 1)], ag_send.at[m])
        take(rs.at[m], rs_send.at[m])
        return carry

    lax.fori_loop(0, MICRO, drained, 0)

    @pl.when(jnp.logical_and(section == 1, half == 1))
    def _():
        feed().wait_send()

    @pl.when(primary)
    def _():
        for copy in sibling_copies():
            copy.wait_send()
        for n in range(4):
            for copy in piece_copies(n, sibling, rows, True):
                copy.wait_send()

    @pl.when(jnp.logical_not(primary))
    def _():
        for n in range(4):
            for copy in piece_copies(n, section, near[n], False):
                copy.wait_send()


def model(x0, gain, w_gate, w_up, w_down, final_gain, head):
    rows_here, width = x0.shape
    r = rows_here // MICRO
    vmem = pl.BlockSpec(memory_space=pltpu.VMEM)
    hbm = pl.BlockSpec(memory_space=pl.ANY)
    dma = pltpu.SemaphoreType.DMA
    return pl.pallas_call(
        model_kernel,
        out_shape=jax.ShapeDtypeStruct((16, 8, 128), jnp.float32),
        in_specs=[vmem, hbm, hbm, hbm, hbm, vmem, vmem],
        out_specs=vmem,
        scratch_shapes=[
            pltpu.VMEM((width, 2 * SPAN), jnp.bfloat16),
            pltpu.VMEM((width, 2 * SPAN), jnp.bfloat16),
            pltpu.VMEM((2 * SPAN, width), jnp.bfloat16),
            pltpu.VMEM((1, width), jnp.float32),
            pltpu.VMEM((MICRO, r, width), jnp.bfloat16),
            pltpu.VMEM((MICRO, GROUP, r, width), jnp.bfloat16),
            pltpu.VMEM((MICRO, GROUP + 1, r, width), jnp.bfloat16),
            pltpu.VMEM((MICRO, GROUP, r, width), jnp.bfloat16),
            pltpu.VMEM((GROUP * r, 2 * SPAN), jnp.bfloat16),
            pltpu.VMEM((8, 128), jnp.float32),
            pltpu.VMEM((8, 128), jnp.float32),
            pltpu.VMEM((16, 8, 128), jnp.float32),
            dma((4,)),
            dma((4,)),
            dma((4,)),
            dma((3, 4)),
            dma((3, 4)),
            dma,
            dma,
            dma((MICRO,)),
            dma((MICRO,)),
            dma((MICRO,)),
            dma((MICRO,)),
            dma,
            dma,
        ],
        compiler_params=pltpu.CompilerParams(
            has_side_effects=True, vmem_limit_bytes=60 * 1024 * 1024
        ),
        name="reward_model",
    )(x0.reshape(MICRO, r, width), gain, w_gate, w_up, w_down, final_gain, head)


def on_device(
    features,
    ages,
    age_table,
    returns,
    owners,
    slots,
    norm_gain,
    w_gate,
    w_up,
    w_down,
    final_gain,
    reward_head,
    old_priority,
):
    sections = lax.axis_size("section")
    section = lax.axis_index("section")
    groups = lax.axis_size("rows")
    group = lax.axis_index("rows")
    table_size = old_priority.shape[0]
    onehot = (ages[:, None] == jnp.arange(age_table.shape[0])[None, :]).astype(jnp.bfloat16)
    entry = (
        features.astype(jnp.float32)
        + jnp.dot(onehot, age_table, preferred_element_type=jnp.float32)
    ).astype(jnp.bfloat16)
    extra = SPAN - w_gate.shape[2]
    everyone = model(
        entry,
        norm_gain,
        jnp.pad(w_gate[0], ((0, 0), (0, extra))),
        jnp.pad(w_up[0], ((0, 0), (0, extra))),
        jnp.pad(w_down[0], ((0, extra), (0, 0))),
        final_gain[None, :],
        reward_head[None, :],
    )
    rewards = everyone[:, 0, :]
    names = (owners[:, 0] * table_size + slots).astype(jnp.float32)
    told = lax.all_gather(jnp.stack([returns, names]), "rows")
    priority = jnp.exp(0.6 * jnp.log(jnp.abs(rewards - told[:, 0]) + 0.05)).reshape(-1)
    named = told[:, 1].reshape(-1)
    share = table_size // sections
    entries = group * table_size + section * share + jnp.arange(share)
    match = named[:, None] == entries[None, :].astype(jnp.float32)
    best = jnp.max(jnp.where(match, priority[:, None], 0.0), axis=0)
    old = lax.dynamic_slice_in_dim(old_priority, section * share, share, 0)
    refreshed = jnp.where(best > 0.0, best, old)
    total = lax.psum(jnp.sum(refreshed), ("rows", "section"))
    weights = refreshed * (table_size * groups / total)
    part = rewards.shape[1] // sections
    rewards_out = lax.dynamic_slice(rewards, (group, section * part), (1, part))[0]
    return (rewards_out, weights)


def solution(mesh):
    placed = (
        P("rows", None),
        P("rows"),
        P(),
        P("rows"),
        P("rows", None),
        P("rows"),
        P("section", None),
        P("section", None, "rows"),
        P("section", None, "rows"),
        P("section", "rows", None),
        P(),
        P(),
        P("rows"),
    )
    return jax.shard_map(
        on_device,
        mesh=mesh,
        in_specs=placed,
        out_specs=(P(("rows", "section")), P(("rows", "section"))),
        check_vma=False,
    )
```

time: 783 us -> 346 us (0.44)
  Pallas kernels: 0 us -> 240 us
  waiting for transfers between devices: 238 us -> 0 us
  blocking collectives: 263 us -> 87.3 us
  starting transfers between devices: 102 us -> 0 us
  matrix products: 87.4 us -> 1.06 us
  other arithmetic: 44.9 us -> 4.33 us
  loops' own time: 20.8 us -> 0 us
    all_to_all x15 -> x0, blocking collectives: 254 us -> none  [from_everyone(): return lax.all_to_all(copies, axis, split_axis=0, concat_axis=0, tiled=True)]
    pallas_call x0 -> x1, Pallas kernels: none -> 240 us  [model(): pl.pallas_call(model_kernel, out_shape=jax.ShapeDtypeStruct((16, 8, 128),...]
    all_to_all x18 -> x0, waiting for transfers between devices: 204 us -> none  [the longest x15 189 us: summed_on_arrival(): parts = lax.all_to_all(cut_along(shard, dim, count), axis, 0, 0, tiled=True)]
    dot_general x30 -> x0, matrix products: 86.1 us -> none  [the longest x15 76.5 us: layer_split(): jnp.dot(hidden, w_down[layer], preferred_element_type=jnp.float32)]
    psum x0 -> x1, blocking collectives: none -> 70.6 us  [on_device(): total = lax.psum(jnp.sum(refreshed), ('rows', 'section'))]
    all_to_all x18 -> x0, starting transfers between devices: 67.3 us -> none  [the longest x15 56.2 us: summed_on_arrival(): parts = lax.all_to_all(cut_along(shard, dim, count), axis, 0, 0, tiled=True)]
    ppermute x15 -> x0, starting transfers between devices: 34.6 us -> none  [shifted(): lax.ppermute(value, axis, [(source, source + steps) for source in range(f...]
    ppermute x15 -> x0, waiting for transfers between devices: 33.7 us -> none  [shifted(): lax.ppermute(value, axis, [(source, source + steps) for source in range(f...]
  transfers between devices with their start and end apart: 33 -> 0, of which waited for: 33 -> 0; matrix products, arithmetic and copies ran while one was open for 0% -> 0% of each run, Pallas kernels for 0% -> 0%
where the time goes in v1:
time: 346 us
  Pallas kernels  240 us (69%)
  blocking collectives  87.3 us (25%)
  local copies, waits for them, and re-layouts  12.3 us (4%)
  other arithmetic  4.33 us (1%)
    pallas_call x1, Pallas kernels, model(): pl.pallas_call(model_kernel, out_shape=jax.ShapeDtypeStruct((16, 8, 128),...  240 us
    psum x1, blocking collectives, on_device(): total = lax.psum(jnp.sum(refreshed), ('rows', 'section'))  70.6 us
    all_gather x1, blocking collectives, on_device(): told = lax.all_gather(jnp.stack([returns, names]), 'rows')  16.8 us

profile of v1, /device:TPU:1, one launch (start us, length us, event | category | flops | bytes accessed | tf_op | source)
XLA Modules:
  0.0 346.0 jit_solution(5313542817102637519)
XLA Ops:
  0.6 0.0 copy-start
  0.7 2.7 copy.21
  3.4 1.5 pad.11.wg_in
  4.9 2.7 copy.22
  7.6 0.0 copy-start.1
  7.6 1.5 pad.12.wu_in
  9.1 0.0 copy-start.2
  9.1 0.0 copy-start.6
  9.1 0.7 copy-done.1
  9.8 0.0 copy-start.3
  9.8 0.0 copy-start.4
  9.8 1.4 pad.13.wd_in
  11.2 0.0 copy-done
  11.2 0.0 copy-done.2
  11.2 0.0 copy-done.6
  11.2 1.1 fusion.1.x0
  12.3 0.0 copy-done.3
  12.3 0.6 broadcast_in_dim.21.final_gain
  12.9 0.0 copy-done.4
  12.9 0.6 broadcast_in_dim.22.head
  13.5 0.0 copy-start.7
  13.5 0.0 copy-start.8
  13.5 0.0 copy-start.5
  13.5 239.5 %reward_model.1 = f32[16,8,128]{2,1,0:T(8,128)} custom-call(bf16[16,8,1536]{2,1,0:T(8,128)(2,1)} %fusion.1.x0, f32[1,1536]{1,0:T(1,128)} %gain_in.1, bf16[1536,640]{1,0:T(8,128)(2,1)} %pad.11.wg_in, bf16[1536,640]{1,0:T(8,128)(2,1)} %pad.12.wu_in, bf16[640,1536]{1,0:T(8,128)(2,1)} %pad.13.wd_in, f32[1,1536]{1,0:T(1,128)} %broadcast_in_dim.21.final_gain, ...), custom_call_target="tpu_custom_call" | custom-call | tf_op jit(solution)/shard_map/reward_model/pallas_call | solution.py:345
  253.0 0.0 copy-done.7
  253.0 0.0 copy-done.8
  253.0 0.0 copy-done.5
  253.1 16.8 %all-gather.1 = f32[16,2,128]{2,1,0:T(2,128)S(1)} all-gather(f32[1,2,128]{2,1,0:T(2,128)S(1)} %maximum_bitcast_fusion), channel_id=2, replica_groups=mesh['section'=8,'rows'=16] {'rows'}, dimensions={0}, use_global_device_ids=true | all-gather | bytes 17408 | tf_op jit(solution)/shard_map/all_gather | solution.py:421
  269.8 0.9 multiply_exponential_fusion
  270.7 0.7 select_reduce_fusion
  271.4 1.4 fusion.6
  272.8 70.6 %psum.7 = f32[]{:T(128)} all-reduce(f32[]{:T(128)} %fusion.6), channel_id=1, replica_groups=mesh['section'=8,'rows'=16] {'rows','section'}, use_global_device_ids=true, to_apply=%region_2.3 | all-reduce | flops 1 | bytes 8 | tf_op jit(solution)/shard_map/psum | solution.py:430
  344.1 1.3 broadcast_multiply_fusion
  345.4 0.6 dynamic-slice_bitcast_fusion
  (3 shorter events, 0.0 us)
Async XLA Ops:
  0.6 10.6 %copy-start = (bf16[16,1536]{1,0:T(8,128)(2,1)S(1)}, bf16[16,1536]{1,0:T(8,128)(2,1)}, u32[]{:S(2)}) copy-start(bf16[16,1536]{1,0:T(8,128)(2,1)} %param.15) | copy-start | bytes 147460
  7.6 2.2 copy-start.1
  9.1 2.1 copy-start.2
  9.1 2.1 copy-start.6
  9.8 2.5 copy-start.3
  9.8 3.1 copy-start.4
  13.5 239.6 %copy-start.7 = (s32[128]{0:T(128)S(1)}, s32[128]{0:T(128)}, u32[]{:S(2)}) copy-start(s32[128]{0:T(128)} %param.18) | copy-start | bytes 1540
  13.5 239.6 %copy-start.8 = (s32[128,1]{0,1:T(1,128)S(1)}, s32[128,1]{0,1:T(1,128)}, u32[]{:S(2)}) copy-start(s32[128,1]{0,1:T(1,128)} %param.17) | copy-start | bytes 1540
  13.5 239.6 %copy-start.5 = (f32[128]{0:T(128)S(1)}, f32[128]{0:T(128)}, u32[]{:S(2)}) copy-start(f32[128]{0:T(128)} %param.16) | copy-start | bytes 1540

commit v2 on v1

v2 whole, which is shorter than its diff:
```python
import functools

import jax
import jax.numpy as jnp
from jax import lax
from jax.experimental import pallas as pl
from jax.experimental.pallas import tpu as pltpu
from jax.sharding import PartitionSpec as P

MESH = pl.DeviceIdType.MESH
MICRO = 16
GROUP = 8
OWN = 560
SPAN = 1152
TABLE = 4096


def place(member, half):
    y = member // 2
    return 4 * y + 2 * (member % 2) + (y + half) % 2


def copy_to(src, dst, send, recv, section, rows):
    return pltpu.make_async_remote_copy(
        src_ref=src,
        dst_ref=dst,
        send_sem=send,
        recv_sem=recv,
        device_id={"section": section, "rows": rows},
        device_id_type=MESH,
    )


FIRST = (((0,), (0,)), ((), ()))


def take(ref, sem):
    pltpu.make_async_copy(ref, ref, sem).wait()


PIECES = ((0, 144), (144, 144), (288, 144), (432, 128))
GATHER_ORDER = ((2, 1), (1, 0), (3, 0), (1, 1), (3, 1), (0, 1), (2, 0))
SCATTER_ORDER = ((2, 0), (2, 1), (1, 1), (3, 1), (1, 0), (3, 0), (0, 0), (0, 1))


def model_kernel(
    features,
    ages,
    age_table,
    returns,
    owners,
    slots,
    gain_in,
    wg_in,
    wu_in,
    wd_in,
    final_gain,
    head,
    old,
    out_rewards,
    out_weights,
    wg_rows,
    wu_rows,
    wg,
    wu,
    wd,
    gain,
    x0,
    xs,
    ag,
    rs,
    ps,
    hid,
    news,
    allrew,
    told,
    sums,
    own_sem,
    w0_send,
    w0_recv,
    w1_send,
    w1_recv,
    x_send,
    x_recv,
    ag_send,
    ag_recv,
    rs_send,
    rs_recv,
    all_send,
    all_recv,
    told_send,
    told_recv,
    sum_send,
    sum_recv,
):
    section = lax.axis_index("section")
    rows = lax.axis_index("rows")
    plane, core = section // 2, section % 2
    y, x = rows // 4, rows % 4
    half = (x + y) % 2
    stage = 2 * plane + half
    member = y * 2 + x // 2
    primary = core == half
    sibling = 2 * plane + 1 - core
    later = (stage + 1) % 8
    later_half = later % 2
    later_section = 2 * (later // 2) + core
    across_section = 2 * ((plane + half + half + 3) % 4) + core
    width = features.shape[-1]
    r = features.shape[0] // MICRO
    block = GROUP * r

    def peer_of(dy, db):
        return 2 * ((y + dy) % 4) + (member + db) % 2

    barrier = pltpu.get_barrier_semaphore()

    def greet(to_section, to_rows):
        pl.semaphore_signal(
            barrier,
            inc=1,
            device_id={"section": to_section, "rows": to_rows},
            device_id_type=MESH,
        )

    for step in range(1, 16):
        greet(section, (rows + step) % 16)
    greet(sibling, rows)
    for k in range(GROUP):
        greet(across_section, place(k, 1 - half))
    pl.semaphore_wait(barrier, 24)

    near = (
        4 * y + (x + 1) % 4,
        4 * y + (x + 3) % 4,
        4 * ((y + 1) % 4) + x,
        4 * ((y + 3) % 4) + x,
    )

    def own_copies():
        return (
            pltpu.make_async_copy(gain_in, gain, own_sem.at[0]),
            pltpu.make_async_copy(wg_in, wg_rows.at[pl.ds(0, OWN)], own_sem.at[1]),
            pltpu.make_async_copy(wu_in, wu_rows.at[pl.ds(0, OWN)], own_sem.at[2]),
            pltpu.make_async_copy(wd_in, wd.at[pl.ds(0, OWN)], own_sem.at[3]),
        )

    def sibling_copies():
        pairs = (
            (gain_in, gain),
            (wg_in, wg_rows.at[pl.ds(0, OWN)]),
            (wu_in, wu_rows.at[pl.ds(0, OWN)]),
            (wd_in, wd.at[pl.ds(0, OWN)]),
        )
        return [
            copy_to(src, dst, w0_send.at[i], w0_recv.at[i], sibling, rows)
            for i, (src, dst) in enumerate(pairs)
        ]

    def piece_copies(n, to_section, to_rows, relay):
        at, size = PIECES[n]
        targets = [ref.at[pl.ds(OWN + at, size)] for ref in (wg_rows, wu_rows, wd)]
        sources = targets if relay else [ref.at[pl.ds(at, size)] for ref in (wg_in, wu_in, wd_in)]
        return [
            copy_to(src, dst, w1_send.at[i, n], w1_recv.at[i, n], to_section, to_rows)
            for i, (src, dst) in enumerate(zip(sources, targets))
        ]

    def feed(part):
        return copy_to(
            x0.at[pl.ds(4 * part, 4)],
            xs.at[pl.ds(4 * part, 4)],
            x_send.at[part],
            x_recv.at[part],
            section,
            place(member, 0),
        )

    feeding = jnp.logical_and(section == 1, half == 1)

    @pl.when(jnp.logical_and(plane == 0, primary))
    def _():
        number = age_table.shape[0]
        level = lax.broadcasted_iota(jnp.int32, (number, features.shape[0]), 0)
        onehot = (level == ages[...]).astype(jnp.float32).astype(jnp.bfloat16)
        aged = lax.dot_general(onehot, age_table[...], FIRST, preferred_element_type=jnp.float32)
        entry = (features[...].astype(jnp.float32) + aged).reshape(MICRO, r, width)
        x0[...] = entry.astype(jnp.bfloat16)

        @pl.when(half == 0)
        def _():
            xs[...] = x0[...]

    @pl.when(feeding)
    def _():
        for part in range(4):
            feed(part).start()

    @pl.when(primary)
    def _():
        for copy in own_copies():
            copy.start()
        for copy in sibling_copies():
            copy.start()

    @pl.when(jnp.logical_not(primary))
    def _():
        for i in range(3):
            for n in range(4):
                piece_copies(n, section, near[n], False)[i].start()

    tail = pl.ds(2 * OWN, SPAN - 2 * OWN)
    for ref in (wg_rows, wu_rows, wd):
        ref[tail, :] = jnp.zeros((SPAN - 2 * OWN, width), jnp.bfloat16)

    def enter(m):
        @pl.when(jnp.logical_and(jnp.logical_and(section == 1, half == 0), m % 4 == 0))
        def _():
            take(xs.at[pl.ds(m, 4)], x_recv.at[m // 4])

        @pl.when(stage > 0)
        def _():
            xs[m] = summed(m)

        wide = xs[m].astype(jnp.float32)
        mean = jnp.mean(wide * wide, axis=-1, keepdims=True)
        ag[m, member] = (wide * lax.rsqrt(mean + 1e-06) * gain[...]).astype(jnp.bfloat16)
        for dy, db in GATHER_ORDER:
            copy_to(
                ag.at[m, member],
                ag.at[m, member],
                ag_send.at[m],
                ag_recv.at[m],
                section,
                place(peer_of(dy, db), half),
            ).start()
        copy_to(
            xs.at[m],
            rs.at[m, GROUP],
            rs_send.at[m],
            rs_recv.at[m],
            later_section,
            place(member, later_half),
        ).start()

    def summed(m):
        take(rs.at[m], rs_recv.at[m])
        total = rs[m, 0].astype(jnp.float32)
        for i in range(1, GROUP + 1):
            total = total + rs[m, i].astype(jnp.float32)
        return total.astype(jnp.bfloat16)

    def layer(m):
        take(ag.at[m, pl.ds(0, GROUP - 1)], ag_recv.at[m])
        normed = ag[m].reshape(block, width)
        for at in range(0, SPAN, 256):
            size = min(256, SPAN - at)
            gate = jnp.dot(normed, wg[:, at : at + size], preferred_element_type=jnp.float32)
            upper = jnp.dot(normed, wu[:, at : at + size], preferred_element_type=jnp.float32)
            hid[:, at : at + size] = (gate * jax.nn.sigmoid(gate) * upper).astype(jnp.bfloat16)
        for at in range(0, width, 256):
            part = jnp.dot(hid[...], wd[:, at : at + 256], preferred_element_type=jnp.float32)
            ps[m, :, :, at : at + 256] = part.astype(jnp.bfloat16).reshape(GROUP, r, 256)
        for dy, db in SCATTER_ORDER:
            peer = peer_of(dy, db)
            copy_to(
                ps.at[m, peer],
                rs.at[m, member],
                rs_send.at[m],
                rs_recv.at[m],
                later_section,
                place(peer, later_half),
            ).start()

    def turned(first, last):
        def turn(i, carry):
            at = pl.multiple_of(i * 128, 128)
            wg[:, pl.ds(at, 128)] = wg_rows[pl.ds(at, 128), :].T
            wu[:, pl.ds(at, 128)] = wu_rows[pl.ds(at, 128), :].T
            return carry

        lax.fori_loop(first, last, turn, 0)

    @pl.when(primary)
    def _():
        own_copies()[0].wait()

    @pl.when(jnp.logical_not(primary))
    def _():
        sibling_copies()[0].wait_recv()

    ahead = jnp.where(stage == 0, 3, 1)

    def early(m, carry):
        enter(m)
        return carry

    @pl.when(stage == 0)
    def _():
        lax.fori_loop(0, ahead, early, 0)

    news[...] = (owners[...] * TABLE + slots[...]).astype(jnp.float32)
    told[rows, 0] = returns[...]
    told[rows, 1] = news[...]
    for step in range(1, 16):
        copy_to(
            told.at[rows],
            told.at[rows],
            told_send,
            told_recv,
            section,
            (rows + step) % 16,
        ).start()

    @pl.when(primary)
    def _():
        for copy in own_copies()[1:]:
            copy.wait()

    @pl.when(jnp.logical_not(primary))
    def _():
        for copy in sibling_copies()[1:]:
            copy.wait_recv()

    turned(0, 4)
    for n in range(4):

        @pl.when(primary)
        def _():
            for copy in piece_copies(n, sibling, rows, True):
                copy.wait_recv()
                copy.start()

        @pl.when(jnp.logical_not(primary))
        def _():
            for copy in piece_copies(n, section, near[n], False):
                copy.wait_recv()

        turned(4 + n, 5 + n if n < 3 else 9)

    @pl.when(stage > 0)
    def _():
        lax.fori_loop(0, ahead, early, 0)

    def tick(m, carry):
        @pl.when(m + ahead < MICRO)
        def _():
            enter(m + ahead)

        layer(m)
        return carry

    lax.fori_loop(0, MICRO, tick, 0)
    take(told.at[pl.ds(0, 15)], told_recv)

    def flat(step):
        target = (section * 16 + rows + step) % 128
        return target // 16, target % 16

    shard = place(member, core)

    @pl.when(stage == 0)
    def _():
        def finish(m, line):
            wide = summed(m).astype(jnp.float32)
            mean = jnp.mean(wide * wide, axis=-1, keepdims=True)
            ready = wide * lax.rsqrt(mean + 1e-06) * final_gain[...]
            value = jnp.sum(ready * head[...], axis=-1, keepdims=True)
            spot = lax.broadcasted_iota(jnp.int32, (r, 128), 0) + m * r
            lane = lax.broadcasted_iota(jnp.int32, (r, 128), 1)
            return line + jnp.where(spot == lane, value, 0.0)

        line = lax.fori_loop(0, MICRO, finish, jnp.zeros((r, 128), jnp.float32))
        allrew[shard] = jnp.sum(line, axis=0, keepdims=True)

        def send(step, carry):
            to_section, to_rows = flat(step)
            copy_to(
                allrew.at[shard], allrew.at[shard], all_send, all_recv, to_section, to_rows
            ).start()
            return carry

        lax.fori_loop(1, 128, send, 0)
        take(allrew.at[pl.ds(0, 15)], all_recv)

    @pl.when(stage > 0)
    def _():
        take(allrew, all_recv)

    out_rewards[...] = allrew[rows]
    share = TABLE // 8
    lane = lax.broadcasted_iota(jnp.int32, (8, 128), 1)
    sub = lax.broadcasted_iota(jnp.int32, (8, 128), 0)
    priority, named = [], []
    for j in range(16):
        gap = jnp.abs(allrew[j] - told[j, 0]) + 0.05
        priority.append(jnp.broadcast_to(jnp.exp(0.6 * jnp.log(gap)), (8, 128)))
        named.append(jnp.broadcast_to(told[j, 1], (8, 128)))
    first = rows * TABLE + section * share
    lines = []
    for q in range(share // 128):
        line = jnp.zeros((8, 128), jnp.float32)
        for g in range(16):
            entry = (first + q * 128 + g * 8 + sub).astype(jnp.float32)
            best = jnp.zeros((8, 128), jnp.float32)
            for j in range(16):
                best = jnp.maximum(best, jnp.where(named[j] == entry, priority[j], 0.0))
            value = jnp.max(best, axis=1, keepdims=True)
            line = line + jnp.where(lane == g * 8 + sub, value, 0.0)
        lines.append(jnp.sum(line, axis=0, keepdims=True))
    kept = old[pl.ds(pl.multiple_of(8 * (section // 2), 8), 8), :]
    total = jnp.zeros((1, 128), jnp.float32)
    for q in range(share // 128):
        before = jnp.where(section % 2 == 0, kept[q : q + 1], kept[q + 4 : q + 5])
        lines[q] = jnp.where(lines[q] > 0.0, lines[q], before)
        total = total + lines[q]
    mine = section * 16 + rows
    sums[mine] = jnp.broadcast_to(jnp.sum(total, axis=1, keepdims=True), (1, 128))

    def send_sum(step, carry):
        to_section, to_rows = flat(step)
        copy_to(
            sums.at[mine], sums.at[mine], sum_send, sum_recv, to_section, to_rows
        ).start()
        return carry

    lax.fori_loop(1, 128, send_sum, 0)

    @pl.when(stage == 0)
    def _():
        take(sums.at[pl.ds(0, 127)], all_send)

    def drained(m, carry):
        take(ag.at[m, pl.ds(0, GROUP - 1)], ag_send.at[m])
        take(rs.at[m], rs_send.at[m])
        return carry

    lax.fori_loop(0, MICRO, drained, 0)
    take(told.at[pl.ds(0, 15)], told_send)

    @pl.when(feeding)
    def _():
        for part in range(4):
            feed(part).wait_send()

    @pl.when(primary)
    def _():
        for copy in sibling_copies():
            copy.wait_send()
        for n in range(4):
            for copy in piece_copies(n, sibling, rows, True):
                copy.wait_send()

    @pl.when(jnp.logical_not(primary))
    def _():
        for n in range(4):
            for copy in piece_copies(n, section, near[n], False):
                copy.wait_send()

    take(sums.at[pl.ds(0, 127)], sum_recv)
    whole = jnp.sum(sums[...], axis=0)
    for q in range(share // 128):
        out_weights[q : q + 1, :] = lines[q] * (float(16 * TABLE) / whole)
    take(sums.at[pl.ds(0, 127)], sum_send)


def on_device(
    features,
    ages,
    age_table,
    returns,
    owners,
    slots,
    norm_gain,
    w_gate,
    w_up,
    w_down,
    final_gain,
    reward_head,
    old_priority,
):
    sections = lax.axis_size("section")
    section = lax.axis_index("section")
    rows_here, width = features.shape
    r = rows_here // MICRO
    vmem = pl.BlockSpec(memory_space=pltpu.VMEM)
    hbm = pl.BlockSpec(memory_space=pl.ANY)
    dma = pltpu.SemaphoreType.DMA
    half, single = jnp.bfloat16, jnp.float32
    line, weights = pl.pallas_call(
        model_kernel,
        out_shape=[
            jax.ShapeDtypeStruct((1, rows_here), single),
            jax.ShapeDtypeStruct((TABLE // sections // 128, 128), single),
        ],
        in_specs=[vmem] * 6 + [hbm] * 4 + [vmem] * 3,
        out_specs=[vmem] * 2,
        scratch_shapes=[
            pltpu.VMEM((SPAN, width), half),
            pltpu.VMEM((SPAN, width), half),
            pltpu.VMEM((width, SPAN), half),
            pltpu.VMEM((width, SPAN), half),
            pltpu.VMEM((SPAN, width), half),
            pltpu.VMEM((1, width), single),
            pltpu.VMEM((MICRO, r, width), half),
            pltpu.VMEM((MICRO, r, width), half),
            pltpu.VMEM((MICRO, GROUP, r, width), half),
            pltpu.VMEM((MICRO, GROUP + 1, r, width), half),
            pltpu.VMEM((MICRO, GROUP, r, width), half),
            pltpu.VMEM((GROUP * r, SPAN), half),
            pltpu.VMEM((1, 128), single),
            pltpu.VMEM((16, 1, 128), single),
            pltpu.VMEM((16, 2, 1, 128), single),
            pltpu.VMEM((128, 1, 128), single),
            dma((4,)),
            dma((4,)),
            dma((4,)),
            dma((3, 4)),
            dma((3, 4)),
            dma((4,)),
            dma((4,)),
            dma((MICRO,)),
            dma((MICRO,)),
            dma((MICRO,)),
            dma((MICRO,)),
            dma,
            dma,
            dma,
            dma,
            dma,
            dma,
        ],
        compiler_params=pltpu.CompilerParams(
            collective_id=0, has_side_effects=True, vmem_limit_bytes=60 * 1024 * 1024
        ),
        name="reward_model",
    )(
        features,
        ages.reshape(1, rows_here),
        age_table,
        returns.reshape(1, rows_here),
        owners.reshape(1, rows_here),
        slots.reshape(1, rows_here),
        norm_gain,
        w_gate[0].T,
        w_up[0].T,
        w_down[0],
        final_gain.reshape(1, width),
        reward_head.reshape(1, width),
        old_priority.reshape(TABLE // 128, 128),
    )
    part = rows_here // sections
    rewards = lax.dynamic_slice_in_dim(line[0], section * part, part, 0)
    return (rewards, weights.reshape(-1))


def solution(mesh):
    placed = (
        P("rows", None),
        P("rows"),
        P(),
        P("rows"),
        P("rows", None),
        P("rows"),
        P("section", None),
        P("section", None, "rows"),
        P("section", None, "rows"),
        P("section", "rows", None),
        P(),
        P(),
        P("rows"),
    )
    return jax.shard_map(
        on_device,
        mesh=mesh,
        in_specs=placed,
        out_specs=(P(("rows", "section")), P(("rows", "section"))),
        check_vma=False,
    )
```

time: 346 us -> 237 us (0.68)
  blocking collectives: 87.3 us -> 0 us
  Pallas kernels: 240 us -> 231 us
  local copies, waits for them, and re-layouts: 12.3 us -> 5.04 us
  other arithmetic: 4.33 us -> 0 us
    psum x1 -> x0, blocking collectives: 70.6 us -> none  [on_device(): total = lax.psum(jnp.sum(refreshed), ('rows', 'section'))]
    all_gather x1 -> x0, blocking collectives: 16.8 us -> none  [on_device(): told = lax.all_gather(jnp.stack([returns, names]), 'rows')]
    pallas_call x1, Pallas kernels: 240 us -> 231 us  [on_device(): pl.pallas_call(model_kernel, out_shape=[jax.ShapeDtypeStruct((1, rows_her...]
    unnamed x20 -> x1, local copies, waits for them, and re-layouts: 6.19 us -> 1.24 us
    pad x3 -> x0, local copies, waits for them, and re-layouts: 4.34 us -> none  [the longest x1 1.47 us: on_device(): jnp.pad(w_gate[0], ((0, 0), (0, extra)))]
where the time goes in v2:
time: 237 us; the launch traced here: 236 us
  Pallas kernels  231 us (97%)
  local copies, waits for them, and re-layouts  5.04 us (2%)
    pallas_call x1, Pallas kernels, on_device(): pl.pallas_call(model_kernel, out_shape=[jax.ShapeDtypeStruct((1, rows_her...  231 us

profile of v2, /device:TPU:1, one launch (start us, length us, event | category | flops | bytes accessed | tf_op | source)
XLA Modules:
  0.0 236.4 jit_solution(9780629491854913127)
XLA Ops:
  0.6 1.3 reshape.33.final_gain
  1.9 1.3 reshape.34.head
  3.2 230.7 %reward_model.1 = (f32[1,128]{1,0:T(1,128)}, f32[4,128]{1,0:T(4,128)}) custom-call(bf16[128,1536]{1,0:T(8,128)(2,1)} %features.1, s32[1,128]{1,0:T(1,128)} %bitcast.20, bf16[16,1536]{1,0:T(8,128)(2,1)} %age_table.1, f32[1,128]{1,0:T(1,128)} %bitcast.21, s32[1,128]{1,0:T(1,128)} %bitcast.22, s32[1,128]{1,0:T(1,128)} %bitcast.23, f32[1,1536]{1,0:T(1,128)} %gain_in.1, ...), custom_call_target="tpu_custom_call" | custom-call | tf_op jit(solution)/shard_map/reward_model/pallas_call | solution.py:490
  233.9 1.2 dynamic-slice_bitcast_fusion
  235.1 1.2 copy.16

commit v3 on v2

--- a/solution.py
+++ b/solution.py
@@ -13,6 +13,7 @@
 OWN = 560
 SPAN = 1152
 TABLE = 4096
+EARLY = 13
 
 
 def place(member, half):
@@ -75,6 +76,9 @@
     allrew,
     told,
     sums,
+    cols,
+    shares,
+    bests,
     own_sem,
     w0_send,
     w0_recv,
@@ -102,9 +106,10 @@
     member = y * 2 + x // 2
     primary = core == half
     sibling = 2 * plane + 1 - core
-    later = (stage + 1) % 8
-    later_half = later % 2
-    later_section = 2 * (later // 2) + core
+    last = stage == 7
+    later_half = 1 - half
+    later_section = jnp.where(last | (half == 0), section, (section + 2) % 8)
+    base = jnp.where(last, MICRO, 0)
     across_section = 2 * ((plane + half + half + 3) % 4) + core
     width = features.shape[-1]
     r = features.shape[0] // MICRO
@@ -166,19 +171,24 @@
             for i, (src, dst) in enumerate(zip(sources, targets))
         ]
 
+    gather_rows = [place(peer_of(dy, db), half) for dy, db in GATHER_ORDER]
+    scatter_peers = [peer_of(dy, db) for dy, db in SCATTER_ORDER]
+    scatter_rows = [place(peer, later_half) for peer in scatter_peers]
+
     def feed(part):
         return copy_to(
             x0.at[pl.ds(4 * part, 4)],
             xs.at[pl.ds(4 * part, 4)],
             x_send.at[part],
             x_recv.at[part],
-            section,
+            1,
             place(member, 0),
         )
 
-    feeding = jnp.logical_and(section == 1, half == 1)
-
-    @pl.when(jnp.logical_and(plane == 0, primary))
+    feeding = jnp.logical_and(section == 7, half == 1)
+    entering = jnp.logical_and(section == 0, half == 0)
+
+    @pl.when(jnp.logical_or(entering, feeding))
     def _():
         number = age_table.shape[0]
         level = lax.broadcasted_iota(jnp.int32, (number, features.shape[0]), 0)
@@ -187,7 +197,7 @@
         entry = (features[...].astype(jnp.float32) + aged).reshape(MICRO, r, width)
         x0[...] = entry.astype(jnp.bfloat16)
 
-        @pl.when(half == 0)
+        @pl.when(entering)
         def _():
             xs[...] = x0[...]
 
@@ -225,28 +235,15 @@
         wide = xs[m].astype(jnp.float32)
         mean = jnp.mean(wide * wide, axis=-1, keepdims=True)
         ag[m, member] = (wide * lax.rsqrt(mean + 1e-06) * gain[...]).astype(jnp.bfloat16)
-        for dy, db in GATHER_ORDER:
+        for to_rows in gather_rows:
             copy_to(
-                ag.at[m, member],
-                ag.at[m, member],
-                ag_send.at[m],
-                ag_recv.at[m],
-                section,
-                place(peer_of(dy, db), half),
+                ag.at[m, member], ag.at[m, member], ag_send.at[m], ag_recv.at[m], section, to_rows
             ).start()
-        copy_to(
-            xs.at[m],
-            rs.at[m, GROUP],
-            rs_send.at[m],
-            rs_recv.at[m],
-            later_section,
-            place(member, later_half),
-        ).start()
 
     def summed(m):
         take(rs.at[m], rs_recv.at[m])
         total = rs[m, 0].astype(jnp.float32)
-        for i in range(1, GROUP + 1):
+        for i in range(1, GROUP):
             total = total + rs[m, i].astype(jnp.float32)
         return total.astype(jnp.bfloat16)
 
@@ -258,28 +255,31 @@
             gate = jnp.dot(normed, wg[:, at : at + size], preferred_element_type=jnp.float32)
             upper = jnp.dot(normed, wu[:, at : at + size], preferred_element_type=jnp.float32)
             hid[:, at : at + size] = (gate * jax.nn.sigmoid(gate) * upper).astype(jnp.bfloat16)
+        ours = lax.broadcasted_iota(jnp.int32, (GROUP, r, 256), 0) == member
         for at in range(0, width, 256):
             part = jnp.dot(hid[...], wd[:, at : at + 256], preferred_element_type=jnp.float32)
-            ps[m, :, :, at : at + 256] = part.astype(jnp.bfloat16).reshape(GROUP, r, 256)
-        for dy, db in SCATTER_ORDER:
-            peer = peer_of(dy, db)
-            copy_to(
-                ps.at[m, peer],
-                rs.at[m, member],
-                rs_send.at[m],
-                rs_recv.at[m],
-                later_section,
-                place(peer, later_half),
-            ).start()
-
-    def turned(first, last):
+            kept = xs[m, :, at : at + 256].astype(jnp.float32)[None]
+            part = part.reshape(GROUP, r, 256) + jnp.where(ours, kept, 0.0)
+            ps[m, :, :, at : at + 256] = part.astype(jnp.bfloat16)
+            if at + 256 in (width // 2, width):
+                span = pl.ds(at + 256 - width // 2, width // 2)
+                for peer, to_rows in zip(scatter_peers, scatter_rows):
+                    copy_to(
+                        ps.at[m, peer, :, span],
+                        rs.at[base + m, member, :, span],
+                        rs_send.at[m],
+                        rs_recv.at[base + m],
+                        later_section,
+                        to_rows,
+                    ).start()
+
+    def turned(source, target):
         def turn(i, carry):
             at = pl.multiple_of(i * 128, 128)
-            wg[:, pl.ds(at, 128)] = wg_rows[pl.ds(at, 128), :].T
-            wu[:, pl.ds(at, 128)] = wu_rows[pl.ds(at, 128), :].T
+            target[:, pl.ds(at, 128)] = source[pl.ds(at, 128), :].T
             return carry
 
-        lax.fori_loop(first, last, turn, 0)
+        lax.fori_loop(0, SPAN // 128, turn, 0)
 
     @pl.when(primary)
     def _():
@@ -322,21 +322,66 @@
         for copy in sibling_copies()[1:]:
             copy.wait_recv()
 
-    turned(0, 4)
-    for n in range(4):
-
-        @pl.when(primary)
-        def _():
-            for copy in piece_copies(n, sibling, rows, True):
+    for i in range(3):
+        for n in range(4):
+
+            @pl.when(primary)
+            def _():
+                copy = piece_copies(n, sibling, rows, True)[i]
                 copy.wait_recv()
                 copy.start()
 
-        @pl.when(jnp.logical_not(primary))
-        def _():
-            for copy in piece_copies(n, section, near[n], False):
-                copy.wait_recv()
-
-        turned(4 + n, 5 + n if n < 3 else 9)
+            @pl.when(jnp.logical_not(primary))
+            def _():
+                piece_copies(n, section, near[n], False)[i].wait_recv()
+
+        if i < 2:
+            turned((wg_rows, wu_rows)[i], (wg, wu)[i])
+
+    share = TABLE // 8
+    parts = share // 128
+    lane = lax.broadcasted_iota(jnp.int32, (8, 128), 1)
+    sub = lax.broadcasted_iota(jnp.int32, (8, 128), 0)
+    first = rows * TABLE + section * share
+    mine = section * 16 + rows
+    side = section % 2
+
+    def before(q):
+        near_old = old[pl.ds(pl.multiple_of(8 * (section // 2), 8), 8), :]
+        return jnp.where(side == 0, near_old[q : q + 1], near_old[q + parts : q + parts + 1])
+
+    def lines():
+        wide = [jnp.broadcast_to(told[j, 1], (8, 128)) for j in range(16)]
+        return wide + [(first + q * 128 + lane).astype(jnp.float32) for q in range(parts)]
+
+    def column(line, m):
+        picked = jnp.where(lane == m * r + sub, jnp.broadcast_to(line, (8, 128)), 0.0)
+        return jnp.broadcast_to(jnp.sum(picked, axis=1, keepdims=True), (8, 128))
+
+    def prepare():
+        take(told.at[pl.ds(0, 15)], told_recv)
+        names = lines()
+
+        def count(j, totals):
+            for m in range(MICRO):
+                col = column(told[j, 1], m)
+                cols[j, m] = col
+                totals = [t + jnp.where(col == name, 1.0, 0.0) for t, name in zip(totals, names)]
+            return totals
+
+        zeros = [jnp.zeros((8, 128), jnp.float32)] * len(names)
+        totals = lax.fori_loop(0, 16, count, zeros)
+        counts = [jnp.sum(t, axis=0, keepdims=True) for t in totals]
+        for j in range(16):
+            shares[j] = 1.0 / counts[j]
+        rest = jnp.zeros((1, 128), jnp.float32)
+        for q in range(parts):
+            rest = rest + jnp.where(counts[16 + q] > 0.0, 0.0, before(q))
+        sums[mine] = jnp.broadcast_to(jnp.sum(rest, axis=1, keepdims=True), (1, 128))
+
+    @pl.when(stage > 3)
+    def _():
+        prepare()
 
     @pl.when(stage > 0)
     def _():
@@ -351,84 +396,68 @@
         return carry
 
     lax.fori_loop(0, MICRO, tick, 0)
-    take(told.at[pl.ds(0, 15)], told_recv)
-
-    def flat(step):
-        target = (section * 16 + rows + step) % 128
-        return target // 16, target % 16
+
+    @pl.when(stage < 4)
+    def _():
+        prepare()
 
     shard = place(member, core)
-
-    @pl.when(stage == 0)
-    def _():
-        def finish(m, line):
-            wide = summed(m).astype(jnp.float32)
-            mean = jnp.mean(wide * wide, axis=-1, keepdims=True)
-            ready = wide * lax.rsqrt(mean + 1e-06) * final_gain[...]
-            value = jnp.sum(ready * head[...], axis=-1, keepdims=True)
-            spot = lax.broadcasted_iota(jnp.int32, (r, 128), 0) + m * r
-            lane = lax.broadcasted_iota(jnp.int32, (r, 128), 1)
-            return line + jnp.where(spot == lane, value, 0.0)
-
-        line = lax.fori_loop(0, MICRO, finish, jnp.zeros((r, 128), jnp.float32))
-        allrew[shard] = jnp.sum(line, axis=0, keepdims=True)
-
-        def send(step, carry):
-            to_section, to_rows = flat(step)
-            copy_to(
-                allrew.at[shard], allrew.at[shard], all_send, all_recv, to_section, to_rows
-            ).start()
+    final = stage == 6
+
+    def everyone(ref, send, recv):
+        def send_one(step, carry):
+            target = lax.rem(mine + step, 128)
+            copy_to(ref, ref, send, recv, lax.div(target, 16), lax.rem(target, 16)).start()
             return carry
 
-        lax.fori_loop(1, 128, send, 0)
-        take(allrew.at[pl.ds(0, 15)], all_recv)
-
-    @pl.when(stage > 0)
-    def _():
-        take(allrew, all_recv)
-
-    out_rewards[...] = allrew[rows]
-    share = TABLE // 8
-    lane = lax.broadcasted_iota(jnp.int32, (8, 128), 1)
-    sub = lax.broadcasted_iota(jnp.int32, (8, 128), 0)
-    priority, named = [], []
-    for j in range(16):
-        gap = jnp.abs(allrew[j] - told[j, 0]) + 0.05
-        priority.append(jnp.broadcast_to(jnp.exp(0.6 * jnp.log(gap)), (8, 128)))
-        named.append(jnp.broadcast_to(told[j, 1], (8, 128)))
-    first = rows * TABLE + section * share
-    lines = []
-    for q in range(share // 128):
-        line = jnp.zeros((8, 128), jnp.float32)
-        for g in range(16):
-            entry = (first + q * 128 + g * 8 + sub).astype(jnp.float32)
-            best = jnp.zeros((8, 128), jnp.float32)
-            for j in range(16):
-                best = jnp.maximum(best, jnp.where(named[j] == entry, priority[j], 0.0))
-            value = jnp.max(best, axis=1, keepdims=True)
-            line = line + jnp.where(lane == g * 8 + sub, value, 0.0)
-        lines.append(jnp.sum(line, axis=0, keepdims=True))
-    kept = old[pl.ds(pl.multiple_of(8 * (section // 2), 8), 8), :]
-    total = jnp.zeros((1, 128), jnp.float32)
-    for q in range(share // 128):
-        before = jnp.where(section % 2 == 0, kept[q : q + 1], kept[q + 4 : q + 5])
-        lines[q] = jnp.where(lines[q] > 0.0, lines[q], before)
-        total = total + lines[q]
-    mine = section * 16 + rows
-    sums[mine] = jnp.broadcast_to(jnp.sum(total, axis=1, keepdims=True), (1, 128))
-
-    def send_sum(step, carry):
-        to_section, to_rows = flat(step)
-        copy_to(
-            sums.at[mine], sums.at[mine], sum_send, sum_recv, to_section, to_rows
-        ).start()
-        return carry
-
-    lax.fori_loop(1, 128, send_sum, 0)
-
-    @pl.when(stage == 0)
-    def _():
-        take(sums.at[pl.ds(0, 127)], all_send)
+        lax.fori_loop(1, 128, send_one, 0)
+
+    def finish(m, line):
+        wide = summed(MICRO + m).astype(jnp.float32)
+        mean = jnp.mean(wide * wide, axis=-1, keepdims=True)
+        ready = wide * lax.rsqrt(mean + 1e-06) * final_gain[...].reshape(1, width)
+        value = jnp.sum(ready * head[...].reshape(1, width), axis=-1, keepdims=True)
+        return line + jnp.where(lane == m * r + sub, value, 0.0)
+
+    def share_rewards(turn, start, stop):
+        @pl.when(final)
+        def _():
+            line = lax.fori_loop(start, stop, finish, jnp.zeros((r, 128), jnp.float32))
+            allrew[turn, shard] = jnp.sum(line, axis=0, keepdims=True)
+            everyone(allrew.at[turn, shard], all_send.at[turn], all_recv.at[turn])
+
+    def await_rewards(turn):
+        @pl.when(final)
+        def _():
+            take(allrew.at[turn, pl.ds(0, 15)], all_recv.at[turn])
+
+        @pl.when(jnp.logical_not(final))
+        def _():
+            take(allrew.at[turn], all_recv.at[turn])
+
+    def priority(turn, j):
+        gap = jnp.abs(allrew[turn, j] - told[j, 0]) + 0.05
+        return jnp.exp(0.6 * jnp.log(gap))
+
+    def largest(best, names, line, j, m):
+        col, value = cols[j, m], column(line, m)
+        return [jnp.maximum(b, jnp.where(col == n, value, 0.0)) for b, n in zip(best, names)]
+
+    share_rewards(0, 0, EARLY)
+    await_rewards(0)
+    everyone(sums.at[mine], sum_send, sum_recv)
+    names = lines()
+
+    def first_round(j, best):
+        line = priority(0, j)
+        for m in range(EARLY):
+            best = largest(best, names, line, j, m)
+        return best
+
+    best = lax.fori_loop(0, 16, first_round, [jnp.zeros((8, 128), jnp.float32)] * len(names))
+    for i, b in enumerate(best):
+        bests[i] = b
+    share_rewards(1, EARLY, MICRO)
 
     def drained(m, carry):
         take(ag.at[m, pl.ds(0, GROUP - 1)], ag_send.at[m])
@@ -457,11 +486,32 @@
             for copy in piece_copies(n, section, near[n], False):
                 copy.wait_send()
 
+    take(sums.at[pl.ds(0, 127)], sum_send)
     take(sums.at[pl.ds(0, 127)], sum_recv)
     whole = jnp.sum(sums[...], axis=0)
-    for q in range(share // 128):
-        out_weights[q : q + 1, :] = lines[q] * (float(16 * TABLE) / whole)
-    take(sums.at[pl.ds(0, 127)], sum_send)
+
+    await_rewards(1)
+    names = lines()
+    best = [bests[i] for i in range(len(names))]
+    for j in range(16):
+        line = priority(1, j)
+        for m in range(EARLY, MICRO):
+            best = largest(best, names, line, j, m)
+    best = [jnp.max(b, axis=0, keepdims=True) for b in best]
+    named = jnp.zeros((1, 128), jnp.float32)
+    for j in range(16):
+        named = named + best[j] * shares[j]
+    whole = whole + jnp.sum(named, axis=1, keepdims=True)
+    for q in range(parts):
+        fresh = jnp.where(best[16 + q] > 0.0, best[16 + q], before(q))
+        out_weights[q : q + 1, :] = fresh * (float(16 * TABLE) / whole)
+    spots = lax.broadcasted_iota(jnp.int32, (1, 128), 1)
+    out_rewards[...] = jnp.where(spots < EARLY * r, allrew[0, rows], allrew[1, rows])
+
+    @pl.when(final)
+    def _():
+        for turn in range(2):
+            take(sums.at[pl.ds(0, 127)], all_send.at[turn])
 
 
 def on_device(
@@ -505,13 +555,16 @@
             pltpu.VMEM((MICRO, r, width), half),
             pltpu.VMEM((MICRO, r, width), half),
             pltpu.VMEM((MICRO, GROUP, r, width), half),
-            pltpu.VMEM((MICRO, GROUP + 1, r, width), half),
+            pltpu.VMEM((2 * MICRO, GROUP, r, width), half),
             pltpu.VMEM((MICRO, GROUP, r, width), half),
             pltpu.VMEM((GROUP * r, SPAN), half),
             pltpu.VMEM((1, 128), single),
-            pltpu.VMEM((16, 1, 128), single),
+            pltpu.VMEM((2, 16, 1, 128), single),
             pltpu.VMEM((16, 2, 1, 128), single),
             pltpu.VMEM((128, 1, 128), single),
+            pltpu.VMEM((16, MICRO, 8, 128), single),
+            pltpu.VMEM((16, 1, 128), single),
+            pltpu.VMEM((16 + TABLE // sections // 128, 8, 128), single),
             dma((4,)),
             dma((4,)),
             dma((4,)),
@@ -522,9 +575,9 @@
             dma((MICRO,)),
             dma((MICRO,)),
             dma((MICRO,)),
-            dma((MICRO,)),
-            dma,
-            dma,
+            dma((2 * MICRO,)),
+            dma((2,)),
+            dma((2,)),
             dma,
             dma,
             dma,
@@ -545,8 +598,8 @@
         w_gate[0].T,
         w_up[0].T,
         w_down[0],
-        final_gain.reshape(1, width),
-        reward_head.reshape(1, width),
+        final_gain,
+        reward_head,
         old_priority.reshape(TABLE // 128, 128),
     )
     part = rows_here // sections

time: 237 us -> 228 us (0.962)
  Pallas kernels: 231 us -> 225 us
  local copies, waits for them, and re-layouts: 5.04 us -> 2.46 us
    pallas_call x1, Pallas kernels: 231 us -> 225 us  [on_device(): pl.pallas_call(model_kernel, out_shape=[jax.ShapeDtypeStruct((1, rows_her...]
    reshape x2 -> x0, local copies, waits for them, and re-layouts: 2.58 us -> none  [the longest x1 1.29 us: on_device(): final_gain.reshape(1, width)]
where the time goes in v3:
time: 228 us
  Pallas kernels  225 us (99%)
  local copies, waits for them, and re-layouts  2.46 us (1%)
    pallas_call x1, Pallas kernels, on_device(): pl.pallas_call(model_kernel, out_shape=[jax.ShapeDtypeStruct((1, rows_her...  225 us

profile of v3, /device:TPU:1, one launch (start us, length us, event | category | flops | bytes accessed | tf_op | source)
XLA Modules:
  0.0 228.0 jit_solution(1400911140755408036)
XLA Ops:
  0.6 224.9 %reward_model.1 = (f32[1,128]{1,0:T(1,128)}, f32[4,128]{1,0:T(4,128)}) custom-call(bf16[128,1536]{1,0:T(8,128)(2,1)} %features.1, s32[1,128]{1,0:T(1,128)} %bitcast.20, bf16[16,1536]{1,0:T(8,128)(2,1)} %age_table.1, f32[1,128]{1,0:T(1,128)} %bitcast.21, s32[1,128]{1,0:T(1,128)} %bitcast.22, s32[1,128]{1,0:T(1,128)} %bitcast.23, f32[1,1536]{1,0:T(1,128)} %gain_in.1, ...), custom_call_target="tpu_custom_call" | custom-call | tf_op jit(solution)/shard_map/reward_model/pallas_call | solution.py:540
  225.5 1.2 dynamic-slice_bitcast_fusion
  226.7 1.2 copy.16

commit v4 on v3

--- a/solution.py
+++ b/solution.py
@@ -13,7 +13,7 @@
 OWN = 560
 SPAN = 1152
 TABLE = 4096
-EARLY = 13
+EARLY = 11
 
 
 def place(member, half):
@@ -79,6 +79,7 @@
     cols,
     shares,
     bests,
+    given,
     own_sem,
     w0_send,
     w0_recv,
@@ -108,7 +109,7 @@
     sibling = 2 * plane + 1 - core
     last = stage == 7
     later_half = 1 - half
-    later_section = jnp.where(last | (half == 0), section, (section + 2) % 8)
+    later_section = jnp.where(half == 0, section, (section + 2) % 8)
     base = jnp.where(last, MICRO, 0)
     across_section = 2 * ((plane + half + half + 3) % 4) + core
     width = features.shape[-1]
@@ -133,8 +134,6 @@
     greet(sibling, rows)
     for k in range(GROUP):
         greet(across_section, place(k, 1 - half))
-    pl.semaphore_wait(barrier, 24)
-
     near = (
         4 * y + (x + 1) % 4,
         4 * y + (x + 3) % 4,
@@ -150,12 +149,18 @@
             pltpu.make_async_copy(wd_in, wd.at[pl.ds(0, OWN)], own_sem.at[3]),
         )
 
+    def other_copies():
+        return [
+            pltpu.make_async_copy(src, given.at[i], own_sem.at[i + 1])
+            for i, src in enumerate((wg_in, wu_in, wd_in))
+        ]
+
     def sibling_copies():
         pairs = (
-            (gain_in, gain),
-            (wg_in, wg_rows.at[pl.ds(0, OWN)]),
-            (wu_in, wu_rows.at[pl.ds(0, OWN)]),
-            (wd_in, wd.at[pl.ds(0, OWN)]),
+            (gain, gain),
+            (wg_rows.at[pl.ds(0, OWN)], wg_rows.at[pl.ds(0, OWN)]),
+            (wu_rows.at[pl.ds(0, OWN)], wu_rows.at[pl.ds(0, OWN)]),
+            (wd.at[pl.ds(0, OWN)], wd.at[pl.ds(0, OWN)]),
         )
         return [
             copy_to(src, dst, w0_send.at[i], w0_recv.at[i], sibling, rows)
@@ -165,7 +170,7 @@
     def piece_copies(n, to_section, to_rows, relay):
         at, size = PIECES[n]
         targets = [ref.at[pl.ds(OWN + at, size)] for ref in (wg_rows, wu_rows, wd)]
-        sources = targets if relay else [ref.at[pl.ds(at, size)] for ref in (wg_in, wu_in, wd_in)]
+        sources = targets if relay else [given.at[i, pl.ds(at, size)] for i in range(3)]
         return [
             copy_to(src, dst, w1_send.at[i, n], w1_recv.at[i, n], to_section, to_rows)
             for i, (src, dst) in enumerate(zip(sources, targets))
@@ -188,6 +193,16 @@
     feeding = jnp.logical_and(section == 7, half == 1)
     entering = jnp.logical_and(section == 0, half == 0)
 
+    @pl.when(primary)
+    def _():
+        for copy in own_copies():
+            copy.start()
+
+    @pl.when(jnp.logical_not(primary))
+    def _():
+        for copy in other_copies():
+            copy.start()
+
     @pl.when(jnp.logical_or(entering, feeding))
     def _():
         number = age_table.shape[0]
@@ -201,27 +216,32 @@
         def _():
             xs[...] = x0[...]
 
-    @pl.when(feeding)
-    def _():
-        for part in range(4):
-            feed(part).start()
-
-    @pl.when(primary)
-    def _():
-        for copy in own_copies():
-            copy.start()
-        for copy in sibling_copies():
-            copy.start()
-
-    @pl.when(jnp.logical_not(primary))
-    def _():
-        for i in range(3):
-            for n in range(4):
-                piece_copies(n, section, near[n], False)[i].start()
-
     tail = pl.ds(2 * OWN, SPAN - 2 * OWN)
     for ref in (wg_rows, wu_rows, wd):
         ref[tail, :] = jnp.zeros((SPAN - 2 * OWN, width), jnp.bfloat16)
+    news[...] = (owners[...] * TABLE + slots[...]).astype(jnp.float32)
+    told[rows, 0] = returns[...]
+    told[rows, 1] = news[...]
+
+    pl.semaphore_wait(barrier, 24)
+
+    @pl.when(jnp.logical_not(primary))
+    def _():
+        for i, copy in enumerate(other_copies()):
+            copy.wait()
+            for n in range(4):
+                piece_copies(n, section, near[n], False)[i].start()
+
+    @pl.when(feeding)
+    def _():
+        for part in range(4):
+            feed(part).start()
+
+    @pl.when(primary)
+    def _():
+        for own, copy in zip(own_copies(), sibling_copies()):
+            own.wait()
+            copy.start()
 
     def enter(m):
         @pl.when(jnp.logical_and(jnp.logical_and(section == 1, half == 0), m % 4 == 0))
@@ -255,6 +275,7 @@
             gate = jnp.dot(normed, wg[:, at : at + size], preferred_element_type=jnp.float32)
             upper = jnp.dot(normed, wu[:, at : at + size], preferred_element_type=jnp.float32)
             hid[:, at : at + size] = (gate * jax.nn.sigmoid(gate) * upper).astype(jnp.bfloat16)
+        to_section = jnp.where(last & (m >= EARLY), section, later_section)
         ours = lax.broadcasted_iota(jnp.int32, (GROUP, r, 256), 0) == member
         for at in range(0, width, 256):
             part = jnp.dot(hid[...], wd[:, at : at + 256], preferred_element_type=jnp.float32)
@@ -269,7 +290,7 @@
                         rs.at[base + m, member, :, span],
                         rs_send.at[m],
                         rs_recv.at[base + m],
-                        later_section,
+                        to_section,
                         to_rows,
                     ).start()
 
@@ -281,27 +302,18 @@
 
         lax.fori_loop(0, SPAN // 128, turn, 0)
 
-    @pl.when(primary)
-    def _():
-        own_copies()[0].wait()
-
     @pl.when(jnp.logical_not(primary))
     def _():
         sibling_copies()[0].wait_recv()
 
-    ahead = jnp.where(stage == 0, 3, 1)
+    begun = jnp.where(stage == 0, 1, 0)
 
     def early(m, carry):
         enter(m)
         return carry
 
-    @pl.when(stage == 0)
-    def _():
-        lax.fori_loop(0, ahead, early, 0)
-
-    news[...] = (owners[...] * TABLE + slots[...]).astype(jnp.float32)
-    told[rows, 0] = returns[...]
-    told[rows, 1] = news[...]
+    lax.fori_loop(0, begun, early, 0)
+
     for step in range(1, 16):
         copy_to(
             told.at[rows],
@@ -312,11 +324,6 @@
             (rows + step) % 16,
         ).start()
 
-    @pl.when(primary)
-    def _():
-        for copy in own_copies()[1:]:
-            copy.wait()
-
     @pl.when(jnp.logical_not(primary))
     def _():
         for copy in sibling_copies()[1:]:
@@ -383,15 +390,10 @@
     def _():
         prepare()
 
-    @pl.when(stage > 0)
-    def _():
-        lax.fori_loop(0, ahead, early, 0)
-
     def tick(m, carry):
-        @pl.when(m + ahead < MICRO)
-        def _():
-            enter(m + ahead)
-
+        start = jnp.maximum(m + jnp.where(m > 0, 1, 0), begun)
+        stop = jnp.minimum(m + 2, MICRO)
+        lax.fori_loop(start, stop, early, 0)
         layer(m)
         return carry
 
@@ -402,15 +404,20 @@
         prepare()
 
     shard = place(member, core)
-    final = stage == 6
+    finals = (stage == 0, stage == 6)
 
     def everyone(ref, send, recv):
-        def send_one(step, carry):
-            target = lax.rem(mine + step, 128)
-            copy_to(ref, ref, send, recv, lax.div(target, 16), lax.rem(target, 16)).start()
+        targets = [2 * ((plane + away) % 4) + side for away in (2, 1, 3, 0) for side in (1 - core, core)]
+
+        def send_row(step, carry):
+            to_rows = lax.rem(rows + step, 16)
+            for to_section in targets:
+                copy_to(ref, ref, send, recv, to_section, to_rows).start()
             return carry
 
-        lax.fori_loop(1, 128, send_one, 0)
+        lax.fori_loop(1, 16, send_row, 0)
+        for to_section in targets[:-1]:
+            copy_to(ref, ref, send, recv, to_section, rows).start()
 
     def finish(m, line):
         wide = summed(MICRO + m).astype(jnp.float32)
@@ -420,18 +427,18 @@
         return line + jnp.where(lane == m * r + sub, value, 0.0)
 
     def share_rewards(turn, start, stop):
-        @pl.when(final)
+        @pl.when(finals[turn])
         def _():
             line = lax.fori_loop(start, stop, finish, jnp.zeros((r, 128), jnp.float32))
             allrew[turn, shard] = jnp.sum(line, axis=0, keepdims=True)
             everyone(allrew.at[turn, shard], all_send.at[turn], all_recv.at[turn])
 
     def await_rewards(turn):
-        @pl.when(final)
+        @pl.when(finals[turn])
         def _():
             take(allrew.at[turn, pl.ds(0, 15)], all_recv.at[turn])
 
-        @pl.when(jnp.logical_not(final))
+        @pl.when(jnp.logical_not(finals[turn]))
         def _():
             take(allrew.at[turn], all_recv.at[turn])
 
@@ -508,9 +515,10 @@
     spots = lax.broadcasted_iota(jnp.int32, (1, 128), 1)
     out_rewards[...] = jnp.where(spots < EARLY * r, allrew[0, rows], allrew[1, rows])
 
-    @pl.when(final)
-    def _():
-        for turn in range(2):
+    for turn in range(2):
+
+        @pl.when(finals[turn])
+        def _():
             take(sums.at[pl.ds(0, 127)], all_send.at[turn])
 
 
@@ -565,6 +573,7 @@
             pltpu.VMEM((16, MICRO, 8, 128), single),
             pltpu.VMEM((16, 1, 128), single),
             pltpu.VMEM((16 + TABLE // sections // 128, 8, 128), single),
+            pltpu.VMEM((3, OWN, width), half),
             dma((4,)),
             dma((4,)),
             dma((4,)),
@@ -603,8 +612,26 @@
         old_priority.reshape(TABLE // 128, 128),
     )
     part = rows_here // sections
-    rewards = lax.dynamic_slice_in_dim(line[0], section * part, part, 0)
-    return (rewards, weights.reshape(-1))
+
+    def hand_over(line_ref, weights_ref, rewards_out, weights_out):
+        turned = pltpu.roll(line_ref[...], (rows_here - section_of() * part) % rows_here, 1)
+        rewards_out[...] = turned[:, :part]
+        weights_out[...] = weights_ref[...]
+
+    def section_of():
+        return lax.axis_index("section")
+
+    rewards, weights = pl.pallas_call(
+        hand_over,
+        out_shape=[
+            jax.ShapeDtypeStruct((1, part), single),
+            jax.ShapeDtypeStruct(weights.shape, single),
+        ],
+        in_specs=[vmem] * 2,
+        out_specs=[vmem] * 2,
+        name="hand_over",
+    )(line, weights)
+    return (rewards.reshape(-1), weights.reshape(-1))
 
 
 def solution(mesh):

time: 228 us -> 217 us (0.952)
  Pallas kernels: 225 us -> 216 us
  local copies, waits for them, and re-layouts: 2.46 us -> 0 us
    pallas_call x1, Pallas kernels: 225 us -> 215 us  [on_device(): pl.pallas_call(model_kernel, out_shape=[jax.ShapeDtypeStruct((1, rows_her...]
where the time goes in v4:
time: 217 us
  Pallas kernels  216 us (100%)
    pallas_call x1, Pallas kernels, on_device(): pl.pallas_call(model_kernel, out_shape=[jax.ShapeDtypeStruct((1, rows_her...  215 us

profile of v4, /device:TPU:1, one launch (start us, length us, event | category | flops | bytes accessed | tf_op | source)
XLA Modules:
  0.0 216.8 jit_solution(15450777998155985267)
XLA Ops:
  0.6 214.9 %reward_model.1 = (f32[1,128]{1,0:T(1,128)}, f32[4,128]{1,0:T(4,128)}) custom-call(bf16[128,1536]{1,0:T(8,128)(2,1)} %features.1, s32[1,128]{1,0:T(1,128)} %bitcast.18, bf16[16,1536]{1,0:T(8,128)(2,1)} %age_table.1, f32[1,128]{1,0:T(1,128)} %bitcast.19, s32[1,128]{1,0:T(1,128)} %bitcast.20, s32[1,128]{1,0:T(1,128)} %bitcast.21, f32[1,1536]{1,0:T(1,128)} %gain_in.1, ...), custom_call_target="tpu_custom_call" | custom-call | tf_op jit(solution)/shard_map/reward_model/pallas_call | solution.py:548
  215.5 1.3 hand_over.1

commit v5 on v4

--- a/solution.py
+++ b/solution.py
@@ -9,11 +9,12 @@
 
 MESH = pl.DeviceIdType.MESH
 MICRO = 16
+SLOTS = 17
 GROUP = 8
 OWN = 560
 SPAN = 1152
 TABLE = 4096
-EARLY = 11
+EARLY = 12
 
 
 def place(member, half):
@@ -110,7 +111,8 @@
     last = stage == 7
     later_half = 1 - half
     later_section = jnp.where(half == 0, section, (section + 2) % 8)
-    base = jnp.where(last, MICRO, 0)
+    base = jnp.where(last, SLOTS, 0)
+    blocks = MICRO - 1 + 2 * core
     across_section = 2 * ((plane + half + half + 3) % 4) + core
     width = features.shape[-1]
     r = features.shape[0] // MICRO
@@ -192,6 +194,7 @@
 
     feeding = jnp.logical_and(section == 7, half == 1)
     entering = jnp.logical_and(section == 0, half == 0)
+    fed = jnp.logical_and(section == 1, half == 0)
 
     @pl.when(primary)
     def _():
@@ -203,7 +206,7 @@
         for copy in other_copies():
             copy.start()
 
-    @pl.when(jnp.logical_or(entering, feeding))
+    @pl.when(entering | feeding | fed)
     def _():
         number = age_table.shape[0]
         level = lax.broadcasted_iota(jnp.int32, (number, features.shape[0]), 0)
@@ -214,7 +217,11 @@
 
         @pl.when(entering)
         def _():
-            xs[...] = x0[...]
+            xs[pl.ds(0, MICRO)] = x0[...]
+
+        @pl.when(fed)
+        def _():
+            xs[MICRO] = x0[MICRO - 1]
 
     tail = pl.ds(2 * OWN, SPAN - 2 * OWN)
     for ref in (wg_rows, wu_rows, wd):
@@ -244,7 +251,7 @@
             copy.start()
 
     def enter(m):
-        @pl.when(jnp.logical_and(jnp.logical_and(section == 1, half == 0), m % 4 == 0))
+        @pl.when(fed & (m % 4 == 0) & (m < MICRO))
         def _():
             take(xs.at[pl.ds(m, 4)], x_recv.at[m // 4])
 
@@ -391,13 +398,13 @@
         prepare()
 
     def tick(m, carry):
-        start = jnp.maximum(m + jnp.where(m > 0, 1, 0), begun)
-        stop = jnp.minimum(m + 2, MICRO)
+        start = jnp.maximum(m + jnp.where(m > 0, 1, 0), begun) + jnp.where((stage == 0) & (m > 0), 1, 0)
+        stop = jnp.minimum(m + jnp.where(stage == 0, 3, 2), blocks)
         lax.fori_loop(start, stop, early, 0)
         layer(m)
         return carry
 
-    lax.fori_loop(0, MICRO, tick, 0)
+    lax.fori_loop(0, blocks, tick, 0)
 
     @pl.when(stage < 4)
     def _():
@@ -419,18 +426,30 @@
         for to_section in targets[:-1]:
             copy_to(ref, ref, send, recv, to_section, rows).start()
 
-    def finish(m, line):
-        wide = summed(MICRO + m).astype(jnp.float32)
+    def rewarded(m, line, at):
+        wide = summed(SLOTS + m).astype(jnp.float32)
         mean = jnp.mean(wide * wide, axis=-1, keepdims=True)
         ready = wide * lax.rsqrt(mean + 1e-06) * final_gain[...].reshape(1, width)
         value = jnp.sum(ready * head[...].reshape(1, width), axis=-1, keepdims=True)
-        return line + jnp.where(lane == m * r + sub, value, 0.0)
+        return line + jnp.where(lane == at * r + sub, value, 0.0)
+
+    def finish(m, line):
+        return rewarded(m, line, m)
 
     def share_rewards(turn, start, stop):
         @pl.when(finals[turn])
         def _():
-            line = lax.fori_loop(start, stop, finish, jnp.zeros((r, 128), jnp.float32))
-            allrew[turn, shard] = jnp.sum(line, axis=0, keepdims=True)
+            empty = jnp.zeros((r, 128), jnp.float32)
+            line = lax.fori_loop(start, stop, finish, empty)
+            allrew[turn, shard, 0] = jnp.sum(line, axis=0, keepdims=True)
+            allrew[turn, shard, 1] = jnp.zeros((1, 128), jnp.float32)
+            if turn:
+
+                @pl.when(core == 1)
+                def _():
+                    spare = rewarded(MICRO, empty, MICRO - 1)
+                    allrew[turn, shard, 1] = jnp.sum(spare, axis=0, keepdims=True)
+
             everyone(allrew.at[turn, shard], all_send.at[turn], all_recv.at[turn])
 
     def await_rewards(turn):
@@ -443,7 +462,10 @@
             take(allrew.at[turn], all_recv.at[turn])
 
     def priority(turn, j):
-        gap = jnp.abs(allrew[turn, j] - told[j, 0]) + 0.05
+        line = allrew[turn, j, 0]
+        if turn and (j // 4 + j) % 2 == 0:
+            line = line + allrew[turn, j ^ 1, 1]
+        gap = jnp.abs(line - told[j, 0]) + 0.05
         return jnp.exp(0.6 * jnp.log(gap))
 
     def largest(best, names, line, j, m):
@@ -464,14 +486,14 @@
     best = lax.fori_loop(0, 16, first_round, [jnp.zeros((8, 128), jnp.float32)] * len(names))
     for i, b in enumerate(best):
         bests[i] = b
-    share_rewards(1, EARLY, MICRO)
+    share_rewards(1, EARLY, MICRO - 1 + core)
 
     def drained(m, carry):
         take(ag.at[m, pl.ds(0, GROUP - 1)], ag_send.at[m])
         take(rs.at[m], rs_send.at[m])
         return carry
 
-    lax.fori_loop(0, MICRO, drained, 0)
+    lax.fori_loop(0, blocks, drained, 0)
     take(told.at[pl.ds(0, 15)], told_send)
 
     @pl.when(feeding)
@@ -513,13 +535,19 @@
         fresh = jnp.where(best[16 + q] > 0.0, best[16 + q], before(q))
         out_weights[q : q + 1, :] = fresh * (float(16 * TABLE) / whole)
     spots = lax.broadcasted_iota(jnp.int32, (1, 128), 1)
-    out_rewards[...] = jnp.where(spots < EARLY * r, allrew[0, rows], allrew[1, rows])
+    spare = jnp.where(half == 0, allrew[1, rows + 1 - 2 * (rows % 2), 1], 0.0)
+    out_rewards[...] = jnp.where(spots < EARLY * r, allrew[0, rows, 0], allrew[1, rows, 0] + spare)
 
     for turn in range(2):
 
         @pl.when(finals[turn])
         def _():
-            take(sums.at[pl.ds(0, 127)], all_send.at[turn])
+            def sent(step, carry):
+                take(allrew.at[turn], all_send.at[turn])
+                return carry
+
+            lax.fori_loop(0, 7, sent, 0)
+            take(allrew.at[turn, pl.ds(0, 15)], all_send.at[turn])
 
 
 def on_device(
@@ -561,13 +589,13 @@
             pltpu.VMEM((SPAN, width), half),
             pltpu.VMEM((1, width), single),
             pltpu.VMEM((MICRO, r, width), half),
-            pltpu.VMEM((MICRO, r, width), half),
-            pltpu.VMEM((MICRO, GROUP, r, width), half),
-            pltpu.VMEM((2 * MICRO, GROUP, r, width), half),
-            pltpu.VMEM((MICRO, GROUP, r, width), half),
+            pltpu.VMEM((SLOTS, r, width), half),
+            pltpu.VMEM((SLOTS, GROUP, r, width), half),
+            pltpu.VMEM((2 * SLOTS, GROUP, r, width), half),
+            pltpu.VMEM((SLOTS, GROUP, r, width), half),
             pltpu.VMEM((GROUP * r, SPAN), half),
             pltpu.VMEM((1, 128), single),
-            pltpu.VMEM((2, 16, 1, 128), single),
+            pltpu.VMEM((2, 16, 2, 1, 128), single),
             pltpu.VMEM((16, 2, 1, 128), single),
             pltpu.VMEM((128, 1, 128), single),
             pltpu.VMEM((16, MICRO, 8, 128), single),
@@ -581,10 +609,10 @@
             dma((3, 4)),
             dma((4,)),
             dma((4,)),
-            dma((MICRO,)),
-            dma((MICRO,)),
-            dma((MICRO,)),
-            dma((2 * MICRO,)),
+            dma((SLOTS,)),
+            dma((SLOTS,)),
+            dma((SLOTS,)),
+            dma((2 * SLOTS,)),
             dma((2,)),
             dma((2,)),
             dma,

time: 217 us -> 217 us (level)
  no operation moved by 1% of the time
where the time goes in v5:
time: 217 us
  Pallas kernels  216 us (100%)
    pallas_call x1, Pallas kernels, on_device(): pl.pallas_call(model_kernel, out_shape=[jax.ShapeDtypeStruct((1, rows_her...  215 us

profile of v5, /device:TPU:1, one launch (start us, length us, event | category | flops | bytes accessed | tf_op | source)
XLA Modules:
  0.0 216.5 jit_solution(2089567654349829398)
XLA Ops:
  0.6 214.6 %reward_model.1 = (f32[1,128]{1,0:T(1,128)}, f32[4,128]{1,0:T(4,128)}) custom-call(bf16[128,1536]{1,0:T(8,128)(2,1)} %features.1, s32[1,128]{1,0:T(1,128)} %bitcast.18, bf16[16,1536]{1,0:T(8,128)(2,1)} %age_table.1, f32[1,128]{1,0:T(1,128)} %bitcast.19, s32[1,128]{1,0:T(1,128)} %bitcast.20, s32[1,128]{1,0:T(1,128)} %bitcast.21, f32[1,1536]{1,0:T(1,128)} %gain_in.1, ...), custom_call_target="tpu_custom_call" | custom-call | tf_op jit(solution)/shard_map/reward_model/pallas_call | solution.py:576
  215.3 1.3 hand_over.1
